TPU v7x, 256 devices: a whole 4x4x8 slice. The times are simulated.
256 devices in a mesh: group: 4 (over x_hi, core), seq: 64 (over x_lo, y, z).
Axes of the slice: x: 4 (x_hi: 2, x_lo: 2; x = x_hi * 2 + x_lo), y: 4, z: 8, core: 2. Of those that a mesh axis runs over, the one named last changes fastest.
Arguments:
- prefill_query: bfloat16 [4, 4096, 8192], P('group', 'seq'), may hold values from -40 to 40
- prefill_key: bfloat16 [4, 4096, 1024], P('group', 'seq'), may hold values from -40 to 40
- prefill_value: bfloat16 [4, 4096, 1024], P('group', 'seq'), may hold values from -6 to 6
- lengths: int32 [4], replicated, may hold values from 1024 to 4096
- verify_query: bfloat16 [512, 4, 8192], P(('group', 'seq')), may hold values from -40 to 40
- verify_key: bfloat16 [512, 4, 1024], P(('group', 'seq')), may hold values from -6 to 6
- verify_value: bfloat16 [512, 4, 1024], P(('group', 'seq')), may hold values from -6 to 6
- owner: int32 [512], replicated, may hold values from 0 to 3
- cached: int32 [512], replicated, may hold values from 1 to 64
Outputs:
- prefill_out: bfloat16 [4, 4096, 8192], P('group', 'seq')
- verify_out: bfloat16 [512, 4, 8192], P(('group', 'seq'))
All inputs are finite; a program needn't handle non-finite values.
Results may differ from a plain program's by a relative error of at most 0.005.
Values may be sent and summed in bfloat16 or wider, within the bound.
No kernel may reach another device: no remote copies, remote signals or barrier semaphores. Data moves between devices by JAX's collectives and lax.ppermute only.
A program may use at most 192 MiB of HBM per device.

v0:
```python
import math

import jax
import jax.numpy as jnp
from jax import lax
from jax.sharding import Mesh
from jax.sharding import PartitionSpec as P

HQ = 64
HK = 8
HD = 128
BLK = 64
GROUP = ("group_0", "group_1")
GROUP_SEQ = ("group_0", "group_1", "seq")


def in_one_piece(arrays, axis, dim, along):
    ends, at = ([], 0)
    for a in arrays[:-1]:
        at += a.shape[along]
        ends.append(at)
    both = jnp.concatenate(arrays, axis=along)
    return tuple(jnp.split(lax.all_gather(both, axis, axis=dim, tiled=True), ends, axis=along))


def from_everyone(array, axis):
    length = lax.axis_size(axis)
    return lax.all_to_all(
        jnp.broadcast_to(array[None], (length, *array.shape)), axis, 0, 0, tiled=True
    )


def in_order(blocks, dim):
    blocks = jnp.moveaxis(blocks, 0, dim)
    lengths = blocks.shape
    return blocks.reshape(*lengths[:dim], lengths[dim] * lengths[dim + 1], *lengths[dim + 2 :])


def whole_of(array, axes, dim):
    far, near = axes
    leading = from_everyone(array, far)
    blocks = jnp.swapaxes(from_everyone(leading, near), 0, 1)
    return in_order(blocks.reshape(-1, *array.shape), dim)


def side_by_side(arrays, axis, dim, along):
    widths = [a.shape[along] for a in arrays]
    both = jnp.concatenate(arrays, axis=along)
    result = whole_of(both, axis, dim)
    return tuple(jnp.split(result, [sum(widths[:k]) for k in range(1, len(widths))], axis=along))


def split_up(array, dim, length):
    before, after = (array.shape[:dim], array.shape[dim + 1 :])
    return jnp.moveaxis(array.reshape(*before, length, -1, *after), dim, 0)


def sum_at_owner(array, axis, dim):
    length = lax.axis_size(axis)
    blocks = lax.all_to_all(split_up(array, dim, length), axis, 0, 0, tiled=True)
    return jnp.sum(blocks.astype(jnp.float32), axis=0)


def online_update(state, scores, allowed, values_block, form):
    highest, summed, mixed = state
    masked = jnp.where(allowed, scores, -1e30)
    new_highest = jnp.maximum(highest, jnp.max(masked, axis=-1))
    weights = jnp.where(allowed, jnp.exp(scores - new_highest[..., None]), 0.0)
    factor = jnp.exp(highest - new_highest)
    summed = summed * factor + jnp.sum(weights, axis=-1)
    mixed = mixed * factor[..., None] + jnp.einsum(
        form, weights.astype(jnp.bfloat16), values_block, preferred_element_type=jnp.float32
    )
    return (new_highest, summed, mixed)


def decode_rows(row_input, fresh_input, owners, cacheds, sources, own_heads, scale):
    row_total = row_input.shape[0]
    steps = row_input.shape[1]
    row_queries = row_input.reshape(row_total, steps, own_heads, HD)
    fresh_keys = fresh_input[..., :HD]
    fresh_values = fresh_input[..., HD:]
    fresh_scores = (
        jnp.einsum("rtqd,rsd->rtqs", row_queries, fresh_keys, preferred_element_type=jnp.float32)
        * scale
    )
    step_order = jnp.arange(steps, dtype=jnp.int32)
    causal = (step_order[None, :] <= step_order[:, None])[None, :, None, :]
    start_rows = (
        jnp.full((row_total, steps, own_heads), -1e30, jnp.float32),
        jnp.zeros((row_total, steps, own_heads), jnp.float32),
        jnp.zeros((row_total, steps, own_heads, HD), jnp.float32),
    )
    highest, summed, mixed = online_update(
        start_rows, fresh_scores, causal, fresh_values, "rtqs,rsd->rtqd"
    )
    state = (highest.reshape(-1), summed.reshape(-1), mixed.reshape(-1, HD))
    flat_queries = row_queries.reshape(-1, HD)
    for index, cache, length_value in sources:
        key_pos = jnp.arange(cache.shape[0], dtype=jnp.int32)
        limit = jnp.where(owners == index, jnp.minimum(cacheds * BLK, length_value), 0)
        limit = jnp.repeat(limit, steps * own_heads)
        scores = (
            jnp.einsum("nd,jd->nj", flat_queries, cache[:, :HD], preferred_element_type=jnp.float32)
            * scale
        )
        allowed = key_pos[None, :] < limit[:, None]
        state = online_update(state, scores, allowed, cache[:, HD:], "nj,jd->nd")
    highest, summed, mixed = state
    return (mixed / summed[:, None]).reshape(row_total, steps, own_heads * HD)


def per_device(
    prefill_query,
    prefill_key,
    prefill_value,
    lengths,
    verify_query,
    verify_key,
    verify_value,
    owner,
    cached,
):
    cycle = lax.axis_size("seq")
    trajs = lax.axis_size(GROUP)
    cycle_pos = lax.axis_index("seq")
    traj_pos = lax.axis_index(GROUP)
    tokens = prefill_query.shape[1]
    group = HQ // HK
    per_head = cycle // HK
    own_heads = HQ // cycle
    scale = HD ** (-0.5)
    length = jnp.sum(jnp.where(jnp.arange(trajs, dtype=jnp.int32) == traj_pos, lengths, 0))
    queries = prefill_query[0].reshape(tokens, HK, group, HD)
    slot_pos = cycle_pos * tokens + jnp.arange(tokens, dtype=jnp.int32)
    start_state = (
        jnp.full((tokens, HK, group), -1e30, jnp.float32),
        jnp.zeros((tokens, HK, group), jnp.float32),
        jnp.zeros((tokens, HK, group, HD), jnp.float32),
    )
    pieces = in_one_piece((prefill_key, prefill_value), "seq", 1, 0)
    key_piece = pieces[0][0]
    value_piece = pieces[1][0]
    count = key_piece.shape[0]
    width = math.gcd(count, 512)
    keys = key_piece.reshape(count // width, width, HK, HD)
    values = value_piece.reshape(count // width, width, HK, HD)
    offsets = width * jnp.arange(count // width, dtype=jnp.int32)

    def advance(carry, inputs):
        key_block, value_block, offset = inputs
        scores = (
            jnp.einsum("tkgd,jkd->tkgj", queries, key_block, preferred_element_type=jnp.float32)
            * scale
        )
        key_pos = offset + jnp.arange(width, dtype=jnp.int32)
        allowed = ((key_pos[None, :] <= slot_pos[:, None]) & (key_pos[None, :] < length))[
            :, None, None, :
        ]
        return (online_update(carry, scores, allowed, value_block, "tkgj,jkd->tkgd"), None)

    state = lax.scan(advance, start_state, (keys, values, offsets))[0]
    paired = jnp.concatenate(
        [prefill_key[0].reshape(tokens, HK, HD), prefill_value[0].reshape(tokens, HK, HD)], axis=-1
    )
    outgoing = jnp.repeat(jnp.transpose(paired, (1, 0, 2)), per_head, axis=0)
    head_cache = lax.all_to_all(outgoing, "seq", split_axis=0, concat_axis=1, tiled=True)
    highest, summed, mixed = state
    prefill_out = (mixed / summed[..., None]).astype(jnp.bfloat16).reshape(1, tokens, HQ * HD)
    local_rows = verify_query.shape[0]
    steps = verify_query.shape[1]
    fresh_pair = jnp.concatenate(
        [
            verify_key.reshape(local_rows, steps, HK, HD),
            verify_value.reshape(local_rows, steps, HK, HD),
        ],
        axis=-1,
    )
    fresh_out = jnp.repeat(fresh_pair, per_head, axis=2).reshape(local_rows, steps, cycle * 2 * HD)
    arrived_query, arrived_fresh = (
        lax.all_to_all(verify_query, "seq", split_axis=2, concat_axis=0, tiled=True),
        lax.all_to_all(fresh_out, "seq", split_axis=2, concat_axis=0, tiled=True),
    )
    every_query, every_fresh = side_by_side(
        (arrived_query, arrived_fresh), ("group_0", "group_1"), 0, 2
    )
    sources = [(traj_pos, head_cache[0], length)]
    decoded = decode_rows(every_query, every_fresh, owner, cached, sources, own_heads, scale)
    decoded = jnp.where((owner == traj_pos)[:, None, None], decoded, 0.0)
    result = sum_at_owner(decoded.astype(jnp.bfloat16), GROUP, 0).astype(jnp.bfloat16)
    verify_out = lax.all_to_all(result, "seq", split_axis=0, concat_axis=2, tiled=True)
    return (prefill_out, verify_out)


def solution(mesh):
    split = Mesh(mesh.devices.reshape(2, 2, mesh.shape["seq"]), ("group_0", "group_1", "seq"))
    placed = (
        P(GROUP, "seq", None),
        P(GROUP, "seq", None),
        P(GROUP, "seq", None),
        P(),
        P(GROUP_SEQ, None, None),
        P(GROUP_SEQ, None, None),
        P(GROUP_SEQ, None, None),
        P(),
        P(),
    )
    return jax.shard_map(
        per_device,
        mesh=split,
        in_specs=placed,
        out_specs=(P(GROUP, "seq", None), P(GROUP_SEQ, None, None)),
        check_vma=False,
    )
```

profile of v0, /device:TPU:6, one launch (start us, length us, event | category | flops | bytes accessed | tf_op | source)
XLA Modules:
  0.0 504.2 jit_solution(16593509621957304161)
XLA Ops:
  7.2 1.7 pad_maximum_fusion.1
  9.0 8.4 %copy.68 = bf16[2,4,8192]{1,0,2:T(2,128)(2,1)} copy(bf16[2,4,8192]{2,1,0:T(4,128)(2,1)} %param.15) | data formatting | bytes 262144 | tf_op args[4]
  17.3 9.3 %reshape.189 = bf16[64,2,512]{2,1,0:T(2,128)(2,1)} reshape(bf16[8192,2,4]{2,1,0:T(2,128)(2,1)} %bitcast.106) | data formatting | bytes 262144
  26.6 13.2 %all-to-all-start = ((bf16[64,2,512]{2,1,0:T(2,128)(2,1)}), bf16[64,2,512]{2,1,0:T(2,128)(2,1)S(1)}, u32[]{:S(2)}, u32[]{:S(2)}) async-start(bf16[64,2,512]{2,1,0:T(2,128)(2,1)} %reshape.189), calls=%async_computation | async-start | bytes 262144 | tf_op jit(solution)/shard_map/all_to_all | solution.py:181
  40.6 5.6 %broadcast_in_dim.133 = bf16[2,4,8,8,256]{1,0,4,3,2:T(2,128)(2,1)} broadcast(bf16[2,4,8,256]{1,0,3,2:T(2,128)(2,1)S(1)} %copy.70), dimensions={0,1,2,4} | broadcast | bytes 294912 | tf_op jit(solution)/shard_map/broadcast_in_dim | solution.py:179
  46.3 16.8 %reshape.187 = bf16[64,2,1024]{2,1,0:T(2,128)(2,1)} reshape(bf16[16384,2,4]{2,1,0:T(2,128)(2,1)} %bitcast.101) | data formatting | bytes 524288
  63.1 11.3 %all-to-all-start.1 = ((bf16[64,2,1024]{2,1,0:T(2,128)(2,1)}), bf16[64,2,1024]{2,1,0:T(2,128)(2,1)S(1)}, u32[]{:S(2)}, u32[]{:S(2)}) async-start(bf16[64,2,1024]{2,1,0:T(2,128)(2,1)} %reshape.187), calls=%async_computation.1 | async-start | bytes 524288 | tf_op jit(solution)/shard_map/all_to_all | solution.py:182
  74.4 10.0 %reshape.190 = bf16[8192,2,4]{2,1,0:T(2,128)(2,1)} reshape(bf16[64,2,512]{2,1,0:T(2,128)(2,1)S(1)} %all-to-all-done) | data formatting | bytes 262144
  84.4 8.6 %copy.69 = bf16[2,4,64,128]{3,0,2,1:T(2,128)(2,1)S(1)} copy(bf16[2,4,64,128]{1,0,3,2:T(2,128)(2,1)} %bitcast.105) | data formatting | bytes 262144 | tf_op jit(solution)/shard_map/all_to_all | solution.py:181
  93.2 19.0 %reshape.188 = bf16[16384,2,4]{2,1,0:T(2,128)(2,1)} reshape(bf16[64,2,1024]{2,1,0:T(2,128)(2,1)S(1)} %all-to-all-done.1) | data formatting | bytes 524288
  112.2 12.0 %copy.85 = bf16[2,4,64,256]{3,2,1,0:T(8,128)(2,1)S(1)} copy(bf16[2,4,64,256]{1,0,3,2:T(2,128)(2,1)} %bitcast.102) | data formatting | bytes 524288 | tf_op jit(solution)/shard_map/all_to_all | solution.py:182
  125.7 4.9 all-to-all-start.2
  130.8 8.1 %all-to-all-done.2 = bf16[2,128,4,384]{3,2,1,0:T(4,128)(2,1)S(1)} async-done(((bf16[2,128,4,384]{3,2,1,0:T(4,128)(2,1)}), bf16[2,128,4,384]{3,2,1,0:T(4,128)(2,1)S(1)}, u32[]{:S(2)}, u32[]{:S(2)}) %all-to-all-start.2) | async-done | bytes 786464 | tf_op jit(solution)/shard_map/all_to_all | solution.py:28
  139.3 5.0 all_to_all.78
  144.3 1.6 broadcast_in_dim.141
  145.9 19.0 %all-to-all-start.4 = ((bf16[64,64,256]{2,1,0:T(8,128)(2,1)}), bf16[64,64,256]{2,1,0:T(8,128)(2,1)}, u32[]{:S(2)}, u32[]{:S(2)}) async-start(bf16[64,64,256]{2,1,0:T(8,128)(2,1)} %bitcast.13), calls=%async_computation.4 | async-start | bytes 4194304 | tf_op jit(solution)/shard_map/all_to_all | solution.py:167
  169.7 1.8 convolution_add_fusion
  171.5 62.4 %all-to-all-done.4 = bf16[64,64,256]{2,1,0:T(8,128)(2,1)} async-done(((bf16[64,64,256]{2,1,0:T(8,128)(2,1)}), bf16[64,64,256]{2,1,0:T(8,128)(2,1)}, u32[]{:S(2)}, u32[]{:S(2)}) %all-to-all-start.4) | async-done | bytes 2097184 | tf_op jit(solution)/shard_map/all_to_all | solution.py:167
  233.9 15.6 %select_reduce_fusion = (f32[2048]{0:T(1024)S(1)}, f32[2048,4096]{1,0:T(8,128)}) fusion(s32[2048]{0:T(1024)S(1)} %lt.30, bf16[2048,128]{1,0:T(8,128)(2,1)S(1)} %bitcast.116, bf16[4096,256]{1,0:T(8,128)(2,1)} %bitcast.14), kind=kOutput, calls=%fused_computation.31 | convolution fusion | flops 2181036032 | bytes 35143680 | tf_op jit(solution)/shard_map/nd,jd->nj/dot_general | solution.py:104
  249.5 15.8 %fusion.19 = f32[2048]{0:T(1024)S(1)} fusion(f32[2048,4096]{1,0:T(8,128)} %get-tuple-element.180, f32[2048]{0:T(1024)S(1)} %get-tuple-element.166, s32[2048]{0:T(1024)S(1)} %lt.30), kind=kLoop, calls=%fused_computation.33 | loop fusion | flops 41940992 | bytes 33579008 | tf_op jit(solution)/shard_map/reduce_sum | solution.py:70
  265.3 15.2 %fusion.26 = bf16[2048,128]{1,0:T(8,128)(2,1)S(1)} fusion(f32[2048,4096]{1,0:T(8,128)} %get-tuple-element.180, f32[2048]{0:T(1024)S(1)} %get-tuple-element.166, s32[2048]{0:T(1024)S(1)} %lt.30, bf16[4096,256]{1,0:T(8,128)(2,1)} %bitcast.14, f32[2048,128]{1,0:T(8,128)S(1)} %bitcast.124, f32[2048]{0:T(1024)S(1)} %multiply_add_fusion, ...), kind=kOutput, calls=%fused_computation.40 | convolution fusion | flops 2190475264 | bytes 36208640 | tf_op jit(solution)/shard_map/nj,jd->nd/dot_general | solution.py:71
  281.4 13.8 %all_to_all.79 = bf16[4,128,4,128]{3,2,1,0:T(4,128)(2,1)S(1)} all-to-all(bf16[4,128,4,128]{3,2,1,0:T(4,128)(2,1)S(1)} %select_convert_fusion), channel_id=1, replica_groups=mesh['group_0'=2,'group_1'=2,'seq'=64] {'group_0','group_1'}, dimensions={0} | all-to-all | bytes 1048576 | tf_op jit(solution)/shard_map/all_to_all | solution.py:60
  296.1 15.7 %all-to-all-start.6 = ((bf16[128,4,128]{2,1,0:T(4,128)(2,1)}), bf16[128,4,128]{2,1,0:T(4,128)(2,1)S(1)}, u32[]{:S(2)}, u32[]{:S(2)}) async-start(bf16[128,4,128]{2,1,0:T(4,128)(2,1)} %reduce_sum.54), calls=%async_computation.6 | async-start | bytes 262144 | tf_op jit(solution)/shard_map/all_to_all | solution.py:191
  311.9 1.5 copy.89
  314.1 9.8 %all-to-all-done.6 = bf16[128,4,128]{2,1,0:T(4,128)(2,1)S(1)} async-done(((bf16[128,4,128]{2,1,0:T(4,128)(2,1)}), bf16[128,4,128]{2,1,0:T(4,128)(2,1)S(1)}, u32[]{:S(2)}, u32[]{:S(2)}) %all-to-all-start.6) | async-done | bytes 131104 | tf_op jit(solution)/shard_map/all_to_all | solution.py:191
  324.6 51.9 %all-gather.2.cloned.1.call-done = bf16[2,4096,1024]{2,1,0:T(8,128)(2,1)} async-done(((bf16[2,64,1024]{2,1,0:T(8,128)(2,1)}), bf16[2,4096,1024]{2,1,0:T(8,128)(2,1)}) %all-gather.2.cloned.1.call-update) | async-done | bytes 16777232 | tf_op jit(solution)/shard_map/all_gather | solution.py:23
  376.5 12.7 %slice_bitcast_fusion = (bf16[512,8,8,128]{3,1,2,0:T(8,128)(2,1)}, bf16[512,8,8,128]{3,1,2,0:T(8,128)(2,1)}) fusion(bf16[2,4096,1024]{2,1,0:T(8,128)(2,1)} %all-gather.2.cloned.1.call-done), kind=kLoop, calls=%fused_computation.36 | loop fusion | bytes 33554432
  389.3 8.8 %copy.90 = bf16[512,8,8,128]{3,2,1,0:T(8,128)(2,1)} copy(bf16[512,8,8,128]{3,1,2,0:T(8,128)(2,1)} %get-tuple-element.173) | data formatting | bytes 16777216
  398.1 8.8 %copy.88 = bf16[512,8,8,128]{3,2,1,0:T(8,128)(2,1)} copy(bf16[512,8,8,128]{3,1,2,0:T(8,128)(2,1)} %get-tuple-element.174) | data formatting | bytes 16777216
  406.8 87.6 %while.15 = (s32[]{:T(128)}, f32[64,8,8]{0,2,1:T(8,128)S(1)}, f32[64,8,8]{0,2,1:T(8,128)S(1)}, f32[64,8,8,128]{3,0,2,1:T(8,128)S(1)}, s32[8]{0:T(128)S(1)}, /*in...) while((s32[]{:T(128)}, f32[64,8,8]{0,2,1:T(8,128)S(1)}, ...), condition=%wide.region_4.5_spmd.clone, body=%wide.region_1.4_spmd.clone.sunk | while | flops 1098470912 | bytes 37099176 | solution.py:162
  409.5 1.7 constant_dynamic-slice_fusion.3
  411.2 1.4 fusion.51
  412.6 2.5 fusion.52
  415.1 2.8 bitcast_add_fusion.2
  420.4 1.7 constant_dynamic-slice_fusion.3
  422.1 1.4 fusion.51
  423.5 2.5 fusion.52
  426.1 2.8 bitcast_add_fusion.2
  431.3 1.7 constant_dynamic-slice_fusion.3
  433.0 1.4 fusion.51
  434.4 2.5 fusion.52
  437.0 2.8 bitcast_add_fusion.2
  442.2 1.7 constant_dynamic-slice_fusion.3
  443.9 1.4 fusion.51
  445.4 2.5 fusion.52
  447.9 2.8 bitcast_add_fusion.2
  453.2 1.7 constant_dynamic-slice_fusion.3
  454.8 1.4 fusion.51
  456.3 2.5 fusion.52
  458.8 2.8 bitcast_add_fusion.2
  464.1 1.7 constant_dynamic-slice_fusion.3
  465.8 1.4 fusion.51
  467.2 2.5 fusion.52
  469.7 2.8 bitcast_add_fusion.2
  475.0 1.7 constant_dynamic-slice_fusion.3
  476.7 1.4 fusion.51
  478.1 2.5 fusion.52
  480.7 2.8 bitcast_add_fusion.2
  484.1 1.2 broadcast_compare_fusion.4
  485.9 1.7 constant_dynamic-slice_fusion.3
  487.6 1.4 fusion.51
  489.1 2.5 fusion.52
  491.6 2.8 bitcast_add_fusion.2
  495.9 1.3 reshape.179
  (128 shorter events, 30.3 us)
Async XLA Ops:
  7.2 32.7 %copy-start.2 = (bf16[2,4,1024]{2,1,0:T(4,128)(2,1)S(1)}, bf16[2,4,1024]{2,1,0:T(4,128)(2,1)}, u32[]{:S(2)}) copy-start(bf16[2,4,1024]{2,1,0:T(4,128)(2,1)} %param.16) | copy-start | bytes 49156
  7.2 32.7 %copy-start.3 = (bf16[2,4,1024]{2,1,0:T(4,128)(2,1)S(1)}, bf16[2,4,1024]{2,1,0:T(4,128)(2,1)}, u32[]{:S(2)}) copy-start(bf16[2,4,1024]{2,1,0:T(4,128)(2,1)} %param.17) | copy-start | bytes 49156
  7.2 369.3 %all-gather.2.cloned.1.call-start = ((), (), s32[]{:S(2)}) async-start(), calls=%async_computation.7 | async-start | bytes 17039360 | tf_op jit(solution)/shard_map/all_gather | solution.py:23
  26.6 36.4 %all-to-all-start = ((bf16[64,2,512]{2,1,0:T(2,128)(2,1)}), bf16[64,2,512]{2,1,0:T(2,128)(2,1)S(1)}, u32[]{:S(2)}, u32[]{:S(2)}) async-start(bf16[64,2,512]{2,1,0:T(2,128)(2,1)} %reshape.189), calls=%async_computation | async-start | bytes 262144 | tf_op jit(solution)/shard_map/all_to_all | solution.py:181
  63.1 30.1 %all-to-all-start.1 = ((bf16[64,2,1024]{2,1,0:T(2,128)(2,1)}), bf16[64,2,1024]{2,1,0:T(2,128)(2,1)S(1)}, u32[]{:S(2)}, u32[]{:S(2)}) async-start(bf16[64,2,1024]{2,1,0:T(2,128)(2,1)} %reshape.187), calls=%async_computation.1 | async-start | bytes 524288 | tf_op jit(solution)/shard_map/all_to_all | solution.py:182
  112.2 18.4 %copy-start = (bf16[1,64,1024]{2,1,0:T(8,128)(2,1)S(1)}, bf16[1,64,1024]{2,1,0:T(8,128)(2,1)}, u32[]{:S(2)}) copy-start(bf16[1,64,1024]{2,1,0:T(8,128)(2,1)} %param.13) | copy-start | bytes 393220
  112.2 18.4 %copy-start.1 = (bf16[1,64,1024]{2,1,0:T(8,128)(2,1)S(1)}, bf16[1,64,1024]{2,1,0:T(8,128)(2,1)}, u32[]{:S(2)}) copy-start(bf16[1,64,1024]{2,1,0:T(8,128)(2,1)} %param.12) | copy-start | bytes 393220
  124.6 40.3 %copy-start.6 = (s32[4]{0:T(128)S(1)}, s32[4]{0:T(128)}, u32[]{:S(2)}) copy-start(s32[4]{0:T(128)} %param.14) | copy-start | bytes 52
  124.6 41.0 %copy-start.4 = (s32[512]{0:T(512)S(1)}, s32[512]{0:T(512)}, u32[]{:S(2)}) copy-start(s32[512]{0:T(512)} %param.19) | copy-start | bytes 6148
  124.6 40.9 %copy-start.5 = (s32[512]{0:T(512)S(1)}, s32[512]{0:T(512)}, u32[]{:S(2)}) copy-start(s32[512]{0:T(512)} %param.18) | copy-start | bytes 6148
  125.7 13.2 %all-to-all-start.2 = ((bf16[2,128,4,384]{3,2,1,0:T(4,128)(2,1)}), bf16[2,128,4,384]{3,2,1,0:T(4,128)(2,1)S(1)}, u32[]{:S(2)}, u32[]{:S(2)}) async-start(bf16[2,128,4,384]{3,2,1,0:T(4,128)(2,1)} %broadcast_in_dim.134), calls=%async_computation.2 | async-start | bytes 1572864 | tf_op jit(solution)/shard_map/all_to_all | solution.py:28
  145.9 87.9 %all-to-all-start.4 = ((bf16[64,64,256]{2,1,0:T(8,128)(2,1)}), bf16[64,64,256]{2,1,0:T(8,128)(2,1)}, u32[]{:S(2)}, u32[]{:S(2)}) async-start(bf16[64,64,256]{2,1,0:T(8,128)(2,1)} %bitcast.13), calls=%async_computation.4 | async-start | bytes 4194304 | tf_op jit(solution)/shard_map/all_to_all | solution.py:167
  249.5 15.8 %copy-start.7 = (f32[512,4,128]{2,1,0:T(4,128)S(1)}, f32[512,4,128]{2,1,0:T(4,128)}, u32[]{:S(2)}) copy-start(f32[512,4,128]{2,1,0:T(4,128)} %convolution_add_fusion) | copy-start | bytes 3145732
  296.1 27.8 %all-to-all-start.6 = ((bf16[128,4,128]{2,1,0:T(4,128)(2,1)}), bf16[128,4,128]{2,1,0:T(4,128)(2,1)S(1)}, u32[]{:S(2)}, u32[]{:S(2)}) async-start(bf16[128,4,128]{2,1,0:T(4,128)(2,1)} %reduce_sum.54), calls=%async_computation.6 | async-start | bytes 262144 | tf_op jit(solution)/shard_map/all_to_all | solution.py:191
Sparse Core Ops, SparseCore 0:
  9.8 366.7 all-gather.1
where the time goes:
time: 514 us; the launch traced here: 504 us
  local copies, waits for them, and re-layouts  150 us (29%)
  waiting for transfers between devices  132 us (26%)
  matrix products  67.3 us (13%)
  starting transfers between devices  64.2 us (12%)
  other arithmetic  56.5 us (11%)
  blocking collectives  18.8 us (4%)
  between operations  14.7 us (3%)
    unnamed x28, local copies, waits for them, and re-layouts  96.1 us
    all_to_all x1, waiting for transfers between devices, per_device(): lax.all_to_all(outgoing, 'seq', split_axis=0, concat_axis=1, tiled=True)  62.4 us
    all_gather x1, waiting for transfers between devices, in_one_piece(): lax.all_gather(both, axis, axis=dim, tiled=True)  51.9 us
    dot_general x10, matrix products, online_update(): jnp.einsum(form, weights.astype(jnp.bfloat16), values_block, preferred_el...  39.6 us
    reduce_sum x10, other arithmetic, online_update(): summed = summed * factor + jnp.sum(weights, axis=-1)  35.9 us
    all_to_all x1, starting transfers between devices, per_device(): lax.all_to_all(outgoing, 'seq', split_axis=0, concat_axis=1, tiled=True)  19 us
    dynamic_slice x16, local copies, waits for them, and re-layouts, per_device(): state = lax.scan(advance, start_state, (keys, values, offsets))[0]  17.9 us
    all_to_all x1, starting transfers between devices, per_device(): lax.all_to_all(result, 'seq', split_axis=0, concat_axis=2, tiled=True)  15.7 us
  transfers between devices with their start and end apart: 6, of which 4 were waited for; matrix products, arithmetic and copies ran while one was open for 30% of the time, Pallas kernels for 0%

commit v1 on v0

v1 whole, which is shorter than its diff:
```python
import jax
import jax.numpy as jnp
from jax import lax
from jax.experimental import pallas as pl
from jax.experimental.pallas import tpu as pltpu
from jax.sharding import Mesh
from jax.sharding import PartitionSpec as P

HQ = 64
HK = 8
HD = 128
BLK = 64
QH = HQ // HK
HEAD_W = QH * HD
FRESH_W = HEAD_W + 2 * HD
XY = ("x", "y")
GXY = ("g", "x", "y")
NEG = -1e30
LOG2E = 1.4426950408889634
COEF = HD ** (-0.5) * LOG2E


def dot_nt(a, b):
    return lax.dot_general(a, b, (((1,), (1,)), ((), ())), preferred_element_type=jnp.float32)


def dot_nn(a, b):
    return lax.dot_general(a, b, (((1,), (0,)), ((), ())), preferred_element_type=jnp.float32)


def lane_groups(x):
    return [x[:, k * 128 : (k + 1) * 128] for k in range(x.shape[1] // 128)]


def fold(op, x):
    parts = lane_groups(x)
    while len(parts) > 1:
        parts = [op(parts[k], parts[k + 1]) for k in range(0, len(parts) - 1, 2)] + (
            [parts[-1]] if len(parts) % 2 else []
        )
    return parts[0]


def softmax_step(s, m_old, l_old, acc_old, v):
    rows = s.shape[0]
    top = jnp.max(fold(jnp.maximum, s), axis=1, keepdims=True)
    if m_old is None:
        m_new = jnp.broadcast_to(top, (rows, 128))
    else:
        m_new = jnp.maximum(m_old, top)
    w = jnp.concatenate([jnp.exp2(part - m_new) for part in lane_groups(s)], axis=1)
    l_new = fold(jnp.add, w)
    mixed = dot_nn(w.astype(jnp.bfloat16), v)
    if m_old is not None:
        factor = jnp.exp2(m_old - m_new)
        l_new = l_old * factor + l_new
        mixed = acc_old * factor + mixed
    return m_new, l_new, mixed


def prefill_kernel(info, q_ref, kv_ref, o_ref, q_s, m_s, l_s, acc_s):
    p = pl.program_id(0)
    z = info[0]
    length = info[1]
    tok = q_ref.shape[1]
    zs = kv_ref.shape[0]
    width = zs * tok
    rows = QH * tok
    for h in range(QH):
        q_s[h * tok : (h + 1) * tok, :] = q_ref[0, :, h * HD : (h + 1) * HD]
    m_s[...] = jnp.full((rows, 128), NEG, jnp.float32)
    l_s[...] = jnp.zeros((rows, 128), jnp.float32)
    acc_s[...] = jnp.zeros((rows, HD), jnp.float32)
    half = rows // 2

    def chunk(j, masked):
        kv = kv_ref[:, j, :, :].reshape(width, 2 * HD)
        k = kv[:, :HD]
        v = kv[:, HD:]
        for part in range(2):
            at = slice(part * half, (part + 1) * half)
            s = dot_nt(q_s[at, :], k) * COEF
            if masked:
                col = lax.broadcasted_iota(jnp.int32, (half, width), 1) + j * width
                row = lax.broadcasted_iota(jnp.int32, (half, width), 0) % tok
                slot = p * width + z * tok + row
                s = jnp.where((col <= slot) & (col < length), s, NEG)
            m, l, acc = softmax_step(s, m_s[at, :], l_s[at, :], acc_s[at, :], v)
            m_s[at, :] = m
            l_s[at, :] = l
            acc_s[at, :] = acc

    full = jnp.minimum(p, length // width)

    def body(j, carry):
        chunk(j, False)
        return carry

    lax.fori_loop(0, full, body, 0)
    chunk(full, True)
    out = acc_s[...] / jnp.sum(l_s[...], axis=1, keepdims=True)
    out = out.astype(o_ref.dtype)
    for h in range(QH):
        o_ref[0, :, h * HD : (h + 1) * HD] = out[h * tok : (h + 1) * tok, :]


def prefill(info, q, kv):
    n, tok, _ = q.shape
    zs = kv.shape[0]
    rows = QH * tok
    return pl.pallas_call(
        prefill_kernel,
        out_shape=jax.ShapeDtypeStruct(q.shape, q.dtype),
        grid_spec=pltpu.PrefetchScalarGridSpec(
            num_scalar_prefetch=1,
            grid=(n,),
            in_specs=[
                pl.BlockSpec((1, tok, HEAD_W), lambda p, info: (p, 0, 0)),
                pl.BlockSpec((zs, n, tok, 2 * HD), lambda p, info: (0, 0, 0, 0)),
            ],
            out_specs=pl.BlockSpec((1, tok, HEAD_W), lambda p, info: (p, 0, 0)),
            scratch_shapes=[
                pltpu.VMEM((rows, HD), jnp.bfloat16),
                pltpu.VMEM((rows, 128), jnp.float32),
                pltpu.VMEM((rows, 128), jnp.float32),
                pltpu.VMEM((rows, HD), jnp.float32),
            ],
        ),
        compiler_params=pltpu.CompilerParams(vmem_limit_bytes=40 * 2**20),
        cost_estimate=pl.CostEstimate(
            flops=20 * 10**9, transcendentals=10**7, bytes_accessed=4 * 2**20
        ),
        name="prefill",
    )(info, q, kv)


def verify_kernel(info, x_ref, pos_row, lim_row, pos_col, kv_ref, o_ref, x_s, lim_s, o_s):
    n_batch = info[0]
    cells = pos_row.shape[1]
    zs, ps, tok, _ = kv_ref.shape
    width = zs * tok
    steps = 4
    cut = 8 * steps
    pick = lax.broadcasted_iota(jnp.int32, (cells, cells), 0) == pos_row[...]
    x = x_ref[...].reshape(cells, FRESH_W)
    x_s[...] = dot_nn(pick.astype(jnp.bfloat16), x).astype(jnp.bfloat16)
    limits = jnp.sum(jnp.where(pick, lim_row[...], 0.0), axis=1, keepdims=True)
    lim_s[...] = jnp.broadcast_to(limits, (cells, 128))
    o_s[...] = jnp.zeros((cells, HEAD_W), jnp.bfloat16)

    def batch(b, carry):
        at = pl.ds(pl.multiple_of(b * cut, cut), cut)
        q = jnp.concatenate([x_s[at, h * HD : (h + 1) * HD] for h in range(QH)], axis=0)
        lim = jnp.concatenate([lim_s[at, :]] * QH, axis=0)
        near = pl.ds(pl.multiple_of((b // 4) * 128, 128), 128)
        fk = x_s[near, HEAD_W : HEAD_W + HD]
        fv = x_s[near, HEAD_W + HD :]
        rows = QH * cut
        col = lax.broadcasted_iota(jnp.int32, (rows, 128), 1) - (b % 4) * cut
        row = lax.broadcasted_iota(jnp.int32, (rows, 128), 0) % cut
        seen = (col <= row) & (col >= row - row % steps)
        s = jnp.where(seen, dot_nt(q, fk) * COEF, NEG)
        state = softmax_step(s, None, None, None, fv)
        lane = lax.broadcasted_iota(jnp.int32, (rows, 128), 1).astype(jnp.float32)

        def chunk(j, state):
            kv = kv_ref[:, j, :, :].reshape(width, 2 * HD)
            s = dot_nt(q, kv[:, :HD]) * COEF
            left = lim - (j * width).astype(jnp.float32)
            s = jnp.concatenate(
                [
                    jnp.where(lane + 128.0 * k < left, part, NEG)
                    for k, part in enumerate(lane_groups(s))
                ],
                axis=1,
            )
            return softmax_step(s, *state, kv[:, HD:])

        count = (info[1 + b] + width - 1) // width
        m, l, acc = lax.fori_loop(0, count, chunk, state)
        out = (acc / jnp.sum(l, axis=1, keepdims=True)).astype(jnp.bfloat16)
        for h in range(QH):
            o_s[at, h * HD : (h + 1) * HD] = out[h * cut : (h + 1) * cut, :]
        return carry

    lax.fori_loop(0, n_batch, batch, 0)
    place = lax.broadcasted_iota(jnp.int32, (cells, cells), 1) == pos_col[...]
    out = dot_nn(place.astype(jnp.bfloat16), o_s[...]).astype(jnp.bfloat16)
    o_ref[...] = out.reshape(o_ref.shape)


def verify(info, x, pos_row, lim_row, pos_col, kv):
    cells = pos_row.shape[1]
    full = lambda a: pl.BlockSpec(a.shape, lambda i, info, n=a.ndim: (0,) * n)
    out = jax.ShapeDtypeStruct((*x.shape[:2], HEAD_W), x.dtype)
    return pl.pallas_call(
        verify_kernel,
        out_shape=out,
        grid_spec=pltpu.PrefetchScalarGridSpec(
            num_scalar_prefetch=1,
            grid=(1,),
            in_specs=[full(a) for a in (x, pos_row, lim_row, pos_col, kv)],
            out_specs=pl.BlockSpec(out.shape, lambda i, info: (0, 0, 0)),
            scratch_shapes=[
                pltpu.VMEM((cells, FRESH_W), jnp.bfloat16),
                pltpu.VMEM((cells, 128), jnp.float32),
                pltpu.VMEM((cells, HEAD_W), jnp.bfloat16),
            ],
        ),
        compiler_params=pltpu.CompilerParams(vmem_limit_bytes=40 * 2**20),
        cost_estimate=pl.CostEstimate(
            flops=4 * 10**9, transcendentals=10**6, bytes_accessed=4 * 2**20
        ),
        name="verify",
    )(info, x, pos_row, lim_row, pos_col, kv)


def pack_kv_kernel(k_ref, v_ref, o_ref):
    for h in range(HK):
        o_ref[h, :, :HD] = k_ref[0, :, h * HD : (h + 1) * HD]
        o_ref[h, :, HD:] = v_ref[0, :, h * HD : (h + 1) * HD]


def pack_kv(k, v):
    tok = k.shape[1]
    return pl.pallas_call(
        pack_kv_kernel,
        out_shape=jax.ShapeDtypeStruct((HK, tok, 2 * HD), k.dtype),
        name="pack_kv",
    )(k, v)


def move_kernel(x_ref, o_ref):
    o_ref[...] = x_ref[...].reshape(o_ref.shape)


def pack_q(q):
    tok = q.shape[1]
    return pl.pallas_call(
        move_kernel,
        out_shape=jax.ShapeDtypeStruct((HK, tok, HEAD_W), q.dtype),
        grid=(HK,),
        in_specs=[pl.BlockSpec((1, tok, HEAD_W), lambda p: (0, 0, p))],
        out_specs=pl.BlockSpec((1, tok, HEAD_W), lambda p: (p, 0, 0)),
        name="pack_q",
    )(q)


def unpack_o(o):
    tok = o.shape[1]
    return pl.pallas_call(
        move_kernel,
        out_shape=jax.ShapeDtypeStruct((1, tok, HK * HEAD_W), o.dtype),
        grid=(HK,),
        in_specs=[pl.BlockSpec((1, tok, HEAD_W), lambda p: (p, 0, 0))],
        out_specs=pl.BlockSpec((1, tok, HEAD_W), lambda p: (0, 0, p)),
        name="unpack_o",
    )(o)


def pack_rows_kernel(q_ref, k_ref, v_ref, o_ref):
    groups = o_ref.shape[0] // HK

    def joined(ref, at):
        return jnp.concatenate(
            [ref[i, :, at].astype(jnp.float32) for i in range(ref.shape[0])], axis=0
        ).astype(o_ref.dtype)

    for h in range(HK):
        q = joined(q_ref, slice(h * HEAD_W, (h + 1) * HEAD_W))
        k = joined(k_ref, slice(h * HD, (h + 1) * HD))
        v = joined(v_ref, slice(h * HD, (h + 1) * HD))
        for g in range(groups):
            o_ref[g * HK + h, :, :HEAD_W] = q
            o_ref[g * HK + h, :, HEAD_W : HEAD_W + HD] = k
            o_ref[g * HK + h, :, HEAD_W + HD :] = v


def pack_rows(q, k, v, groups):
    return pl.pallas_call(
        pack_rows_kernel,
        out_shape=jax.ShapeDtypeStruct((groups * HK, q.shape[0] * q.shape[1], FRESH_W), q.dtype),
        name="pack_rows",
    )(q, k, v)


def sum_rows_kernel(x_ref, o_ref):
    groups = x_ref.shape[0] // HK
    steps = o_ref.shape[1]
    for h in range(HK):
        total = x_ref[h].astype(jnp.float32)
        for g in range(1, groups):
            total = total + x_ref[g * HK + h].astype(jnp.float32)
        for i in range(o_ref.shape[0]):
            o_ref[i, :, h * HEAD_W : (h + 1) * HEAD_W] = total[
                i * steps : (i + 1) * steps, :
            ].astype(o_ref.dtype)


def sum_rows(x, rows, steps):
    return pl.pallas_call(
        sum_rows_kernel,
        out_shape=jax.ShapeDtypeStruct((rows, steps, HK * HEAD_W), x.dtype),
        name="sum_rows",
    )(x)


def tables(owner, cached, length, g, z, groups, per, zs, rows, steps):
    own = lax.dynamic_index_in_dim(owner.reshape(groups, per, zs, rows), z, 2, False).reshape(-1)
    held = lax.dynamic_index_in_dim(cached.reshape(groups, per, zs, rows), z, 2, False).reshape(-1)
    limit = jnp.where(own == g, jnp.minimum(held * BLK, length), 0)
    n = limit.shape[0]
    index = jnp.arange(n, dtype=jnp.int32)
    ahead = (limit[None, :] > limit[:, None]) | (
        (limit[None, :] == limit[:, None]) & (index[None, :] < index[:, None])
    )
    rank = jnp.sum(ahead.astype(jnp.int32), axis=1)
    pos = (rank[:, None] * steps + jnp.arange(steps, dtype=jnp.int32)[None, :]).reshape(-1)
    mine = jnp.repeat(limit > 0, steps)
    firsts = jnp.arange(n // 8, dtype=jnp.int32) * 8
    tops = jnp.sum(jnp.where(rank[None, :] == firsts[:, None], limit[None, :], 0), axis=1)
    n_batch = jnp.sum((tops > 0).astype(jnp.int32))
    info = jnp.concatenate([n_batch[None], tops])
    pos_row = pos[None, :]
    lim_row = jnp.repeat(limit, steps).astype(jnp.float32)[None, :]
    pos_col = jnp.where(mine, pos, -1)[:, None]
    return info, pos_row, lim_row, pos_col


def per_device(
    prefill_query,
    prefill_key,
    prefill_value,
    lengths,
    verify_query,
    verify_key,
    verify_value,
    owner,
    cached,
):
    groups = lax.axis_size("g")
    zs = lax.axis_size("z")
    per = lax.axis_size(XY)
    g = lax.axis_index("g")
    z = lax.axis_index("z")
    rows, steps, _ = verify_query.shape
    length = jnp.sum(jnp.where(jnp.arange(groups, dtype=jnp.int32) == g, lengths, 0))

    kv = lax.all_to_all(pack_kv(prefill_key, prefill_value), XY, 0, 0, tiled=True)
    kv_all = lax.all_gather(kv, "z", axis=0, tiled=False)

    q_in, x_in, _ = lax.optimization_barrier(
        (
            pack_q(prefill_query),
            pack_rows(verify_query, verify_key, verify_value, groups),
            kv,
        )
    )
    x = lax.all_to_all(x_in, GXY, 0, 0, tiled=True)
    q = lax.all_to_all(q_in, XY, 0, 0, tiled=True)

    info, pos_row, lim_row, pos_col = tables(
        owner, cached, length, g, z, groups, per, zs, rows, steps
    )
    decoded = verify(info, x, pos_row, lim_row, pos_col, kv_all)
    returned = lax.all_to_all(decoded, GXY, 0, 0, tiled=True)
    out = prefill(jnp.stack([z, length]).astype(jnp.int32), q, kv_all)
    out = lax.all_to_all(out, XY, 0, 0, tiled=True)
    return unpack_o(out), sum_rows(returned, rows, steps)


def solution(mesh):
    split = Mesh(mesh.devices.reshape(4, 2, 4, 8), ("g", "x", "y", "z"))
    token = P("g", ("x", "y", "z"), None)
    row = P(("g", "x", "y", "z"), None, None)
    return jax.shard_map(
        per_device,
        mesh=split,
        in_specs=(token, token, token, P(), row, row, row, P(), P()),
        out_specs=(token, row),
        check_vma=False,
    )
```

time: 514 us -> 143 us (0.28)
  the two profiles are of different devices: /device:TPU:6 before, /device:TPU:32 now
where the time goes in v1:
time: 143 us; the launch traced here: 145 us
  Pallas kernels  54.1 us (38%)
  waiting for transfers between devices  27.6 us (19%)
  starting transfers between devices  26 us (18%)
  between operations  14.2 us (10%)
  blocking collectives  12.7 us (9%)
  local copies, waits for them, and re-layouts  6.27 us (4%)
  other arithmetic  4.53 us (3%)
    pallas_call x1, Pallas kernels, prefill(): pl.pallas_call(prefill_kernel, out_shape=jax.ShapeDtypeStruct(q.shape, q....  30.4 us
    all_to_all x1, blocking collectives, per_device(): lax.all_to_all(pack_kv(prefill_key, prefill_value), XY, 0, 0, tiled=True)  12.7 us
    all_to_all x1, waiting for transfers between devices, per_device(): x = lax.all_to_all(x_in, GXY, 0, 0, tiled=True)  12.3 us
    all_to_all x1, starting transfers between devices, per_device(): returned = lax.all_to_all(decoded, GXY, 0, 0, tiled=True)  12.1 us
    all_to_all x1, waiting for transfers between devices, per_device(): out = lax.all_to_all(out, XY, 0, 0, tiled=True)  8.82 us
    pallas_call x1, Pallas kernels, verify(): pl.pallas_call(verify_kernel, out_shape=out, grid_spec=pltpu.PrefetchScal...  8.06 us
    all_gather x1, waiting for transfers between devices, per_device(): kv_all = lax.all_gather(kv, 'z', axis=0, tiled=False)  6.49 us
    all_to_all x1, starting transfers between devices, per_device(): out = lax.all_to_all(out, XY, 0, 0, tiled=True)  5.47 us
  transfers between devices with their start and end apart: 5, of which 3 were waited for; matrix products, arithmetic and copies ran while one was open for 5% of the time, Pallas kernels for 33%

profile of v1, /device:TPU:32, one launch (start us, length us, event | category | flops | bytes accessed | tf_op | source)
XLA Modules:
  0.0 145.4 jit_solution(5584985238971836902)
XLA Ops:
  7.2 0.0 all-gather.3.cloned.1.call-start
  7.2 1.7 %pack_kv.1 = bf16[8,64,256]{2,1,0:T(8,128)(2,1)} custom-call(bf16[1,64,1024]{2,1,0:T(8,128)(2,1)} %k_ref.3, bf16[1,64,1024]{2,1,0:T(8,128)(2,1)} %v_ref.3), custom_call_target="tpu_custom_call" | custom-call | tf_op jit(solution)/shard_map/pack_kv/pallas_call | solution.py:226
  8.9 12.7 %all_to_all.25 = bf16[8,64,256]{2,1,0:T(8,128)(2,1)} all-to-all(bf16[8,64,256]{2,1,0:T(8,128)(2,1)} %pack_kv.1), channel_id=1, replica_groups=mesh['g'=4,'x'=2,'y'=4,'z'=8] {'x','y'}, dimensions={0} | all-to-all | bytes 524288 | tf_op jit(solution)/shard_map/all_to_all | solution.py:349
  21.7 0.0 all-gather.3.cloned.1.call-update
  21.7 0.8 reshape.123
  22.5 0.8 reshape.124
  23.3 1.3 fusion.3
  24.6 0.7 fusion.2
  25.4 0.1 select_n.45
  25.5 5.2 %pack_q.1 = bf16[8,64,1024]{2,1,0:T(8,128)(2,1)} custom-call(bf16[1,64,8192]{2,1,0:T(8,128)(2,1)} %x_ref.1), custom_call_target="tpu_custom_call" | custom-call | tf_op jit(solution)/shard_map/pack_q/pallas_call | solution.py:239
  30.7 1.8 %pack_rows.1 = bf16[32,8,1280]{2,1,0:T(8,128)(2,1)} custom-call(bf16[2,4,8192]{2,1,0:T(4,128)(2,1)} %q_ref.1, bf16[2,4,1024]{2,1,0:T(4,128)(2,1)} %k_ref.2, bf16[2,4,1024]{2,1,0:T(4,128)(2,1)} %v_ref.2), custom_call_target="tpu_custom_call" | custom-call | tf_op jit(solution)/shard_map/pack_rows/pallas_call | solution.py:280
  32.5 0.2 convert_reduce_fusion
  32.6 4.8 %all-to-all-start.3 = ((bf16[32,8,1280]{2,1,0:T(8,128)(2,1)}), bf16[32,8,1280]{2,1,0:T(8,128)(2,1)S(1)}, u32[]{:S(2)}, u32[]{:S(2)}) async-start(bf16[32,8,1280]{2,1,0:T(8,128)(2,1)} %pack_rows.1), calls=%async_computation.3 | async-start | bytes 1310720 | tf_op jit(solution)/shard_map/all_to_all | solution.py:359
  37.4 0.1 broadcast_select_fusion
  37.5 0.1 select_n.49.pos_col
  37.6 0.1 add.41.pos_row
  37.7 0.1 broadcast_in_dim.53
  37.8 0.1 convert_element_type.23.lim_row
  37.9 12.3 %all-to-all-done.3.x_ref = bf16[32,8,1280]{2,1,0:T(8,128)(2,1)S(1)} async-done(((bf16[32,8,1280]{2,1,0:T(8,128)(2,1)}), bf16[32,8,1280]{2,1,0:T(8,128)(2,1)S(1)}, u32[]{:S(2)}, u32[]{:S(2)}) %all-to-all-start.3) | async-done | bytes 655392 | tf_op jit(solution)/shard_map/all_to_all | solution.py:359
  50.2 3.6 %all-to-all-start.1 = ((bf16[8,64,1024]{2,1,0:T(8,128)(2,1)}), bf16[8,64,1024]{2,1,0:T(8,128)(2,1)S(1)}, u32[]{:S(2)}, u32[]{:S(2)}) async-start(bf16[8,64,1024]{2,1,0:T(8,128)(2,1)} %pack_q.1), calls=%async_computation.1 | async-start | bytes 2097152 | tf_op jit(solution)/shard_map/all_to_all | solution.py:360
  53.8 0.2 select_reduce_fusion
  53.9 0.6 fusion.4
  54.6 0.7 pad_add_fusion.1.info
  55.3 0.7 pad_add_fusion.info
  56.0 6.5 %all-gather.3.cloned.1.call-done = bf16[64,64,256]{2,1,0:T(8,128)(2,1)} async-done(((bf16[8,64,256]{2,1,0:T(8,128)(2,1)}), bf16[64,64,256]{2,1,0:T(8,128)(2,1)}) %all-gather.3.cloned.1.call-update) | async-done | bytes 2097168 | tf_op jit(solution)/shard_map/all_gather | solution.py:350
  62.5 0.0 copy-start
  62.5 1.6 %copy-done = bf16[64,64,256]{2,1,0:T(8,128)(2,1)S(1)} copy-done((bf16[64,64,256]{2,1,0:T(8,128)(2,1)S(1)}, bf16[64,64,256]{2,1,0:T(8,128)(2,1)}, u32[]{:S(2)}) %copy-start) | copy-done | bytes 2097176
  64.1 8.1 %verify.1 = bf16[32,8,1024]{2,1,0:T(8,128)(2,1)} custom-call(s32[9]{0:T(128)S(1)} %pad_add_fusion.1.info, bf16[32,8,1280]{2,1,0:T(8,128)(2,1)S(1)} %all-to-all-done.3.x_ref, s32[1,256]{1,0:T(1,128)S(1)} %add.41.pos_row, f32[1,256]{1,0:T(1,128)S(1)} %convert_element_type.23.lim_row, s32[256,1]{1,0:T(8,128)S(1)} %select_n.49.pos_col, ...), custom_call_target="tpu_custom_call" | custom-call | flops 4000000000 | bytes 4194304 | tf_op jit(solution)/shard_map/verify/pallas_call | solution.py:196
  72.1 0.0 all-to-all-done.1.q_ref
  72.1 12.1 %all-to-all-start.4 = ((bf16[32,8,1024]{2,1,0:T(8,128)(2,1)}), bf16[32,8,1024]{2,1,0:T(8,128)(2,1)S(1)}, u32[]{:S(2)}, u32[]{:S(2)}) async-start(bf16[32,8,1024]{2,1,0:T(8,128)(2,1)} %verify.1), calls=%async_computation.4 | async-start | bytes 1048576 | tf_op jit(solution)/shard_map/all_to_all | solution.py:366
  84.3 0.0 copy-start.1
  84.3 1.6 %copy-done.1 = bf16[64,64,256]{2,1,0:T(8,128)(2,1)S(1)} copy-done((bf16[64,64,256]{2,1,0:T(8,128)(2,1)S(1)}, bf16[64,64,256]{2,1,0:T(8,128)(2,1)}, u32[]{:S(2)}) %copy-start.1) | copy-done | bytes 2097176
  85.9 30.4 %prefill.1 = bf16[8,64,1024]{2,1,0:T(8,128)(2,1)} custom-call(s32[2]{0:T(128)S(1)} %pad_add_fusion.info, bf16[8,64,1024]{2,1,0:T(8,128)(2,1)S(1)} %all-to-all-done.1.q_ref, bf16[8,8,64,256]{3,2,1,0:T(8,128)(2,1)S(1)} %bitcast.5), custom_call_target="tpu_custom_call" | custom-call | flops 20000000000 | bytes 4194304 | tf_op jit(solution)/shard_map/prefill/pallas_call | solution.py:111
  116.3 0.0 all-to-all-done.4.x_ref
  116.3 0.0 copy-start.3
  116.3 5.5 %all-to-all-start.2 = ((bf16[8,64,1024]{2,1,0:T(8,128)(2,1)}), bf16[8,64,1024]{2,1,0:T(8,128)(2,1)S(1)}, u32[]{:S(2)}, u32[]{:S(2)}) async-start(bf16[8,64,1024]{2,1,0:T(8,128)(2,1)} %prefill.1), calls=%async_computation.2 | async-start | bytes 2097152 | tf_op jit(solution)/shard_map/all_to_all | solution.py:368
  121.8 0.0 copy-done.3
  121.8 1.8 %sum_rows.1 = bf16[2,4,8192]{2,1,0:T(4,128)(2,1)} custom-call(bf16[32,8,1024]{2,1,0:T(8,128)(2,1)} %copy-done.3), custom_call_target="tpu_custom_call" | custom-call | tf_op jit(solution)/shard_map/sum_rows/pallas_call | solution.py:301
  123.6 8.8 %all-to-all-done.2.x_ref = bf16[8,64,1024]{2,1,0:T(8,128)(2,1)S(1)} async-done(((bf16[8,64,1024]{2,1,0:T(8,128)(2,1)}), bf16[8,64,1024]{2,1,0:T(8,128)(2,1)S(1)}, u32[]{:S(2)}, u32[]{:S(2)}) %all-to-all-start.2) | async-done | bytes 1048608 | tf_op jit(solution)/shard_map/all_to_all | solution.py:368
  132.4 0.0 copy-start.2
  132.4 1.0 copy-done.2
  133.4 5.2 %unpack_o.1 = bf16[1,64,8192]{2,1,0:T(8,128)(2,1)} custom-call(bf16[8,64,1024]{2,1,0:T(8,128)(2,1)} %copy-done.2), custom_call_target="tpu_custom_call" | custom-call | tf_op jit(solution)/shard_map/unpack_o/pallas_call | solution.py:251
  (4 shorter events, 0.0 us)
Async XLA Ops:
  7.2 55.3 %all-gather.3.cloned.1.call-start = ((), (), s32[]{:S(2)}) async-start(), calls=%async_computation.5 | async-start | bytes 2359296 | tf_op jit(solution)/shard_map/all_gather | solution.py:350
  32.6 17.5 %all-to-all-start.3 = ((bf16[32,8,1280]{2,1,0:T(8,128)(2,1)}), bf16[32,8,1280]{2,1,0:T(8,128)(2,1)S(1)}, u32[]{:S(2)}, u32[]{:S(2)}) async-start(bf16[32,8,1280]{2,1,0:T(8,128)(2,1)} %pack_rows.1), calls=%async_computation.3 | async-start | bytes 1310720 | tf_op jit(solution)/shard_map/all_to_all | solution.py:359
  50.2 22.0 %all-to-all-start.1 = ((bf16[8,64,1024]{2,1,0:T(8,128)(2,1)}), bf16[8,64,1024]{2,1,0:T(8,128)(2,1)S(1)}, u32[]{:S(2)}, u32[]{:S(2)}) async-start(bf16[8,64,1024]{2,1,0:T(8,128)(2,1)} %pack_q.1), calls=%async_computation.1 | async-start | bytes 2097152 | tf_op jit(solution)/shard_map/all_to_all | solution.py:360
  62.5 1.6 %copy-start = (bf16[64,64,256]{2,1,0:T(8,128)(2,1)S(1)}, bf16[64,64,256]{2,1,0:T(8,128)(2,1)}, u32[]{:S(2)}) copy-start(bf16[64,64,256]{2,1,0:T(8,128)(2,1)} %all-gather.3.cloned.1.call-done) | copy-start | bytes 6291460
  72.1 44.2 %all-to-all-start.4 = ((bf16[32,8,1024]{2,1,0:T(8,128)(2,1)}), bf16[32,8,1024]{2,1,0:T(8,128)(2,1)S(1)}, u32[]{:S(2)}, u32[]{:S(2)}) async-start(bf16[32,8,1024]{2,1,0:T(8,128)(2,1)} %verify.1), calls=%async_computation.4 | async-start | bytes 1048576 | tf_op jit(solution)/shard_map/all_to_all | solution.py:366
  84.3 1.6 %copy-start.1 = (bf16[64,64,256]{2,1,0:T(8,128)(2,1)S(1)}, bf16[64,64,256]{2,1,0:T(8,128)(2,1)}, u32[]{:S(2)}) copy-start(bf16[64,64,256]{2,1,0:T(8,128)(2,1)} %all-gather.3.cloned.1.call-done) | copy-start | bytes 6291460
  116.3 5.5 %copy-start.3 = (bf16[32,8,1024]{2,1,0:T(8,128)(2,1)}, bf16[32,8,1024]{2,1,0:T(8,128)(2,1)S(1)}, u32[]{:S(2)}) copy-start(bf16[32,8,1024]{2,1,0:T(8,128)(2,1)S(1)} %all-to-all-done.4.x_ref) | copy-start | bytes 1572868
  116.3 16.1 %all-to-all-start.2 = ((bf16[8,64,1024]{2,1,0:T(8,128)(2,1)}), bf16[8,64,1024]{2,1,0:T(8,128)(2,1)S(1)}, u32[]{:S(2)}, u32[]{:S(2)}) async-start(bf16[8,64,1024]{2,1,0:T(8,128)(2,1)} %prefill.1), calls=%async_computation.2 | async-start | bytes 2097152 | tf_op jit(solution)/shard_map/all_to_all | solution.py:368
  132.4 1.0 copy-start.2
Sparse Core Ops, SparseCore 0:
  21.8 40.6 all-gather.2

commit v2 on v1

v2 whole, which is shorter than its diff:
```python
import functools

import jax
import jax.numpy as jnp
from jax import lax
from jax.experimental import pallas as pl
from jax.experimental.pallas import tpu as pltpu
from jax.sharding import Mesh
from jax.sharding import PartitionSpec as P

HQ = 64
HK = 8
HD = 128
BLK = 64
N_Z = 8
STEPS = 4
BATCH = 16
QH = HQ // HK
HEAD_W = QH * HD
FRESH_W = HEAD_W + 2 * HD
XY = ("x", "y")
GXY = ("g", "x", "y")
NEG = -1e30
LOG2E = 1.4426950408889634
COEF = HD ** (-0.5) * LOG2E


def dot_nt(a, b):
    return lax.dot_general(a, b, (((1,), (1,)), ((), ())), preferred_element_type=jnp.float32)


def dot_nn(a, b):
    return lax.dot_general(a, b, (((1,), (0,)), ((), ())), preferred_element_type=jnp.float32)


def lane_groups(x):
    return [x[:, k * 128 : (k + 1) * 128] for k in range(x.shape[1] // 128)]


def fold(op, x):
    parts = lane_groups(x)
    while len(parts) > 1:
        parts = [op(parts[k], parts[k + 1]) for k in range(0, len(parts) - 1, 2)] + (
            [parts[-1]] if len(parts) % 2 else []
        )
    return parts[0]


def split_scaled(q):
    x = q.astype(jnp.float32) * COEF
    high = x.astype(jnp.bfloat16)
    return jnp.concatenate([high, (x - high.astype(jnp.float32)).astype(jnp.bfloat16)], axis=1)


def score(q2, k):
    return dot_nt(q2, jnp.concatenate([k, k], axis=1))


def softmax_step(s, m_old, acc_old, v):
    top = jnp.max(fold(jnp.maximum, s), axis=1, keepdims=True)
    m_new = jnp.broadcast_to(top, (s.shape[0], 128)) if m_old is None else jnp.maximum(m_old, top)
    w = jnp.concatenate([jnp.exp2(part - m_new) for part in lane_groups(s)], axis=1)
    mixed = dot_nn(w.astype(jnp.bfloat16), jnp.concatenate([v, jnp.ones_like(v)], axis=1))
    if m_old is not None:
        factor = jnp.exp2(m_old - m_new)
        mixed = acc_old * jnp.concatenate([factor, factor], axis=1) + mixed
    return m_new, mixed


def key_slots(segments, z, zs, tok, span):
    width = sum(n for _, _, n in segments)
    col = lax.broadcasted_iota(jnp.int32, (1, span * width), 1)
    at = jnp.zeros((1, span * width), jnp.int32)
    off = 0
    for block in range(span):
        for shift, start, n in segments:
            base = ((z - shift) & (zs - 1)) * tok + block * zs * tok + start - off
            at = jnp.where((col >= off) & (col < off + n), col + base, at)
            off += n
    return at


def joined_blocks(refs, j, span, part):
    return jnp.concatenate([ref[j + i, :, part] for i in range(span) for ref in refs], axis=0)


KEYS = slice(0, HD)
VALUES = slice(HD, 2 * HD)


def prefill_kernel(segments, info, q_ref, *refs):
    n = len(segments)
    kv_refs = refs[:n]
    o_ref, q_s, m_s, acc_s, sa, sb = refs[n:]
    z = info[0]
    length = info[1]
    count, tok, _ = q_ref.shape
    rows = QH * tok
    block = N_Z * tok
    edge = length // block

    def split(p):
        for h in range(QH):
            q_s[p, h * tok : (h + 1) * tok, :] = split_scaled(q_ref[p, :, h * HD : (h + 1) * HD])

    def fill(s_ref, p, j):
        s_ref[...] = score(q_s[p], joined_blocks(kv_refs, j, 1, KEYS))

    def begin(s_ref, p):
        j = jnp.minimum(p, edge)
        at = key_slots(segments, z, N_Z, tok, 1) + j * block
        row = lax.broadcasted_iota(jnp.int32, (rows, 1), 0) % tok
        end = jnp.minimum(p * block + z * tok + row, length - 1)
        s = jnp.where(at <= end, s_ref[...], NEG)
        v = joined_blocks(kv_refs, j, 1, VALUES)
        m_s[p], acc_s[p] = softmax_step(s, None, None, v)

    def take(s_ref, p, j):
        v = joined_blocks(kv_refs, j, 1, VALUES)
        m_s[p], acc_s[p] = softmax_step(s_ref[...], m_s[p], acc_s[p], v)

    def item(t):
        return info[2 + 2 * t], info[3 + 2 * t]

    split(0)
    fill(sa, 0, 0)

    def edges(i, carry):
        p = 2 * i
        split(p + 1)
        fill(sb, p + 1, jnp.minimum(p + 1, edge))
        begin(sa, p)
        split(p + 2)
        fill(sa, p + 2, jnp.minimum(p + 2, edge))
        begin(sb, p + 1)
        return carry

    lax.fori_loop(0, count // 2 - 1, edges, 0)
    split(count - 1)
    fill(sb, count - 1, jnp.minimum(count - 1, edge))
    begin(sa, count - 2)
    fill(sa, *item(0))
    begin(sb, count - 1)

    def body(i, carry):
        fill(sb, *item(2 * i + 1))
        take(sa, *item(2 * i))
        fill(sa, *item(2 * i + 2))
        take(sb, *item(2 * i + 1))
        return carry

    cols = jnp.minimum(edge, count - 1)
    items = (count - 1) * cols - cols * (cols - 1) // 2
    lax.fori_loop(0, items // 2, body, 0)

    @pl.when(items % 2 == 1)
    def _():
        take(sa, *item(items - 1))

    def finish(p, carry):
        out = (acc_s[p, :, :HD] / acc_s[p, :, HD:]).astype(o_ref.dtype)
        for h in range(QH):
            o_ref[p, :, h * HD : (h + 1) * HD] = out[h * tok : (h + 1) * tok, :]
        return carry

    lax.fori_loop(0, count, finish, 0)


def open_items(count):
    pairs = [(p, j) for j in range(count - 1) for p in range(j + 1, count)] + [(1, 0)] * 2
    return [k for pair in pairs for k in pair]


def whole(shape):
    return pl.BlockSpec(shape, lambda i, info: (0,) * len(shape))


def prefill(info, q, kvs, segments):
    n, tok, _ = q.shape
    rows = QH * tok
    return pl.pallas_call(
        functools.partial(prefill_kernel, tuple(segments)),
        out_shape=jax.ShapeDtypeStruct(q.shape, q.dtype),
        grid_spec=pltpu.PrefetchScalarGridSpec(
            num_scalar_prefetch=1,
            grid=(1,),
            in_specs=[whole(a.shape) for a in (q, *kvs)],
            out_specs=whole(q.shape),
            scratch_shapes=[
                pltpu.VMEM((n, rows, 2 * HD), jnp.bfloat16),
                pltpu.VMEM((n, rows, 128), jnp.float32),
                pltpu.VMEM((n, rows, 2 * HD), jnp.float32),
                pltpu.VMEM((rows, N_Z * tok), jnp.float32),
                pltpu.VMEM((rows, N_Z * tok), jnp.float32),
            ],
        ),
        compiler_params=pltpu.CompilerParams(vmem_limit_bytes=40 * 2**20),
        cost_estimate=pl.CostEstimate(
            flops=20 * 10**9, transcendentals=10**7, bytes_accessed=4 * 2**20
        ),
        name="prefill",
    )(info, q, *kvs)


def verify_kernel(segments, info, x_ref, pos_row, lim_row, pos_col, *refs):
    n = len(segments)
    kv_refs = refs[:n]
    o_ref, x_s, lim_s, o_s, q_s, m_s, acc_s, sa, sb = refs[n:]
    z = info[0]
    n_batch = info[1]
    cells = pos_row.shape[1]
    blocks, tok, _ = kv_refs[0].shape
    width = N_Z * tok
    cut = BATCH * STEPS
    rows = QH * cut
    pick = lax.broadcasted_iota(jnp.int32, (cells, cells), 0) == pos_row[...]
    x = x_ref[...].reshape(cells, FRESH_W)
    x_s[...] = dot_nn(pick.astype(jnp.bfloat16), x).astype(jnp.bfloat16)
    limits = jnp.sum(jnp.where(pick, lim_row[...], 0.0), axis=1, keepdims=True)
    lim_s[...] = jnp.broadcast_to(limits, (cells, 128))
    o_s[...] = jnp.zeros((cells, HEAD_W), jnp.bfloat16)
    places = lane_groups(key_slots(segments, z, N_Z, tok, 1).astype(jnp.float32))

    def batch(b, carry):
        at = pl.ds(pl.multiple_of(b * cut, cut), cut)
        for h in range(QH):
            q_s[h * cut : (h + 1) * cut, :] = split_scaled(x_s[at, h * HD : (h + 1) * HD])
        near = pl.ds(pl.multiple_of(b * cut // 128 * 128, 128), 128)
        col = lax.broadcasted_iota(jnp.int32, (1, 128), 1) - b * cut % 128
        row = lax.broadcasted_iota(jnp.int32, (rows, 1), 0) % cut
        seen = (col <= row) & (col >= row - row % STEPS)
        s = jnp.where(seen, score(q_s[...], x_s[near, HEAD_W : HEAD_W + HD]), NEG)
        m_s[...], acc_s[...] = softmax_step(s, None, None, x_s[near, HEAD_W + HD :])

        def fill(s_ref, j):
            k = joined_blocks(kv_refs, jnp.minimum(j, blocks - 1), 1, KEYS)
            s_ref[...] = score(q_s[...], k)

        def take(s_ref, j):
            left = jnp.concatenate([lim_s[at, :]] * QH, axis=0)
            left = left - (j * width).astype(jnp.float32)
            parts = [
                jnp.where(place < left, part, NEG)
                for place, part in zip(places, lane_groups(s_ref[...]))
            ]
            s = jnp.concatenate(parts, axis=1)
            v = joined_blocks(kv_refs, j, 1, VALUES)
            m_s[...], acc_s[...] = softmax_step(s, m_s[...], acc_s[...], v)

        count = (info[2 + b] + width - 1) // width
        fill(sa, 0)

        def body(i, carry):
            fill(sb, 2 * i + 1)
            take(sa, 2 * i)
            fill(sa, 2 * i + 2)
            take(sb, 2 * i + 1)
            return carry

        lax.fori_loop(0, count // 2, body, 0)

        @pl.when(count % 2 == 1)
        def _():
            take(sa, count - 1)

        out = (acc_s[:, :HD] / acc_s[:, HD:]).astype(jnp.bfloat16)
        for h in range(QH):
            o_s[at, h * HD : (h + 1) * HD] = out[h * cut : (h + 1) * cut, :]
        return carry

    lax.fori_loop(0, n_batch, batch, 0)
    place = lax.broadcasted_iota(jnp.int32, (cells, cells), 1) == pos_col[...]
    out = dot_nn(place.astype(jnp.bfloat16), o_s[...]).astype(jnp.bfloat16)
    o_ref[...] = out.reshape(o_ref.shape)


def verify(info, x, pos_row, lim_row, pos_col, kvs, segments):
    cells = pos_row.shape[1]
    rows = QH * BATCH * STEPS
    width = N_Z * kvs[0].shape[1]
    operands = (x, pos_row, lim_row, pos_col, *kvs)
    out = jax.ShapeDtypeStruct((*x.shape[:2], HEAD_W), x.dtype)
    return pl.pallas_call(
        functools.partial(verify_kernel, tuple(segments)),
        out_shape=out,
        grid_spec=pltpu.PrefetchScalarGridSpec(
            num_scalar_prefetch=1,
            grid=(1,),
            in_specs=[whole(a.shape) for a in operands],
            out_specs=whole(out.shape),
            scratch_shapes=[
                pltpu.VMEM((cells, FRESH_W), jnp.bfloat16),
                pltpu.VMEM((cells, 128), jnp.float32),
                pltpu.VMEM((cells, HEAD_W), jnp.bfloat16),
                pltpu.VMEM((rows, 2 * HD), jnp.bfloat16),
                pltpu.VMEM((rows, 128), jnp.float32),
                pltpu.VMEM((rows, 2 * HD), jnp.float32),
                pltpu.VMEM((rows, width), jnp.float32),
                pltpu.VMEM((rows, width), jnp.float32),
            ],
        ),
        compiler_params=pltpu.CompilerParams(vmem_limit_bytes=40 * 2**20),
        cost_estimate=pl.CostEstimate(
            flops=4 * 10**9, transcendentals=10**6, bytes_accessed=4 * 2**20
        ),
        name="verify",
    )(info, *operands)


def pack_kv_kernel(k_ref, v_ref, o_ref):
    for h in range(HK):
        o_ref[h, :, :HD] = k_ref[0, :, h * HD : (h + 1) * HD]
        o_ref[h, :, HD:] = v_ref[0, :, h * HD : (h + 1) * HD]


def pack_kv(k, v):
    tok = k.shape[1]
    return pl.pallas_call(
        pack_kv_kernel,
        out_shape=jax.ShapeDtypeStruct((HK, tok, 2 * HD), k.dtype),
        name="pack_kv",
    )(k, v)


def pack_q_kernel(x_ref, o_ref):
    for h in range(HK):
        o_ref[h] = x_ref[0, :, h * HEAD_W : (h + 1) * HEAD_W]


def pack_q(q):
    return pl.pallas_call(
        pack_q_kernel,
        out_shape=jax.ShapeDtypeStruct((HK, q.shape[1], HEAD_W), q.dtype),
        name="pack_q",
    )(q)


def unpack_o_kernel(x_ref, o_ref):
    for h in range(HK):
        o_ref[0, :, h * HEAD_W : (h + 1) * HEAD_W] = x_ref[h]


def unpack_o(o):
    return pl.pallas_call(
        unpack_o_kernel,
        out_shape=jax.ShapeDtypeStruct((1, o.shape[1], HK * HEAD_W), o.dtype),
        name="unpack_o",
    )(o)


def pack_rows_kernel(q_ref, k_ref, v_ref, o_ref):
    groups = o_ref.shape[0] // HK

    def joined(ref, at):
        return jnp.concatenate(
            [ref[i, :, at].astype(jnp.float32) for i in range(ref.shape[0])], axis=0
        ).astype(o_ref.dtype)

    for h in range(HK):
        q = joined(q_ref, slice(h * HEAD_W, (h + 1) * HEAD_W))
        k = joined(k_ref, slice(h * HD, (h + 1) * HD))
        v = joined(v_ref, slice(h * HD, (h + 1) * HD))
        for g in range(groups):
            o_ref[g * HK + h, :, :HEAD_W] = q
            o_ref[g * HK + h, :, HEAD_W : HEAD_W + HD] = k
            o_ref[g * HK + h, :, HEAD_W + HD :] = v


def pack_rows(q, k, v, groups):
    return pl.pallas_call(
        pack_rows_kernel,
        out_shape=jax.ShapeDtypeStruct((groups * HK, q.shape[0] * q.shape[1], FRESH_W), q.dtype),
        name="pack_rows",
    )(q, k, v)


def sum_rows_kernel(x_ref, o_ref):
    groups = x_ref.shape[0] // HK
    steps = o_ref.shape[1]
    for h in range(HK):
        total = x_ref[h].astype(jnp.float32)
        for g in range(1, groups):
            total = total + x_ref[g * HK + h].astype(jnp.float32)
        for i in range(o_ref.shape[0]):
            o_ref[i, :, h * HEAD_W : (h + 1) * HEAD_W] = total[
                i * steps : (i + 1) * steps, :
            ].astype(o_ref.dtype)


def sum_rows(x, rows, steps):
    return pl.pallas_call(
        sum_rows_kernel,
        out_shape=jax.ShapeDtypeStruct((rows, steps, HK * HEAD_W), x.dtype),
        name="sum_rows",
    )(x)


def tables(owner, cached, length, g, z, groups, per, zs, rows, steps):
    own = lax.dynamic_index_in_dim(owner.reshape(groups, per, zs, rows), z, 2, False).reshape(-1)
    held = lax.dynamic_index_in_dim(cached.reshape(groups, per, zs, rows), z, 2, False).reshape(-1)
    limit = jnp.where(own == g, jnp.minimum(held * BLK, length), 0)
    n = limit.shape[0]
    index = jnp.arange(n, dtype=jnp.int32)
    ahead = (limit[None, :] > limit[:, None]) | (
        (limit[None, :] == limit[:, None]) & (index[None, :] < index[:, None])
    )
    rank = jnp.sum(ahead.astype(jnp.int32), axis=1)
    pos = (rank[:, None] * steps + jnp.arange(steps, dtype=jnp.int32)[None, :]).reshape(-1)
    mine = jnp.repeat(limit > 0, steps)
    firsts = jnp.arange(n // BATCH, dtype=jnp.int32) * BATCH
    tops = jnp.sum(jnp.where(rank[None, :] == firsts[:, None], limit[None, :], 0), axis=1)
    n_batch = jnp.sum((tops > 0).astype(jnp.int32))
    info = jnp.concatenate([z[None], n_batch[None], tops]).astype(jnp.int32)
    pos_row = pos[None, :]
    lim_row = jnp.repeat(limit, steps).astype(jnp.float32)[None, :]
    pos_col = jnp.where(mine, pos, -1)[:, None]
    return info, pos_row, lim_row, pos_col


def per_device(
    prefill_query,
    prefill_key,
    prefill_value,
    lengths,
    verify_query,
    verify_key,
    verify_value,
    owner,
    cached,
):
    groups = lax.axis_size("g")
    zs = lax.axis_size("z")
    per = lax.axis_size(XY)
    g = lax.axis_index("g")
    z = lax.axis_index("z")
    rows, steps, _ = verify_query.shape
    tok = prefill_query.shape[1]
    half = tok // 2
    length = jnp.sum(jnp.where(jnp.arange(groups, dtype=jnp.int32) == g, lengths, 0))

    def along(array, shift):
        return lax.ppermute(array, "z", [(i, (i + shift) % zs) for i in range(zs)])

    def exchange(array, axes):
        return lax.all_to_all(array, axes, 0, 0, tiled=True)

    own = exchange(pack_kv(prefill_key, prefill_value), XY)
    q_in = pack_q(prefill_query)
    x_in = pack_rows(verify_query, verify_key, verify_value, groups)
    q = exchange(q_in, XY)
    up1, down1 = along(own, 1), along(own, -1)
    x = exchange(x_in, GXY)
    up2, down2 = along(up1, 1), along(down1, -1)
    up3, down3 = along(up2, 1), along(down2, -1)
    up4 = along(up2[:, :half], 2)
    down4 = along(down2[:, half:], -2)
    kvs = [own, up1, down1, up2, down2, up3, down3, up4, down4]
    segments = [(s, 0, tok) for s in (0, 1, -1, 2, -2, 3, -3)]
    segments += [(4, 0, half), (4, half, half)]

    where = jnp.concatenate(
        [jnp.stack([z, length]), jnp.array(open_items(per), dtype=jnp.int32)]
    ).astype(jnp.int32)
    info, pos_row, lim_row, pos_col = tables(
        owner, cached, length, g, z, groups, per, zs, rows, steps
    )
    decoded = verify(info, x, pos_row, lim_row, pos_col, kvs, segments)
    returned = exchange(decoded, GXY)
    out = prefill(where, q, kvs, segments)
    out = exchange(out, XY)
    return unpack_o(out), sum_rows(returned, rows, steps)


def solution(mesh):
    split = Mesh(mesh.devices.reshape(4, 2, 4, N_Z), ("g", "x", "y", "z"))
    token = P("g", ("x", "y", "z"), None)
    row = P(("g", "x", "y", "z"), None, None)
    return jax.shard_map(
        per_device,
        mesh=split,
        in_specs=(token, token, token, P(), row, row, row, P(), P()),
        out_specs=(token, row),
        check_vma=False,
    )
```

time: 143 us -> 113 us (0.79); the launches traced: 145 us -> 112 us
  Pallas kernels: 54.1 us -> 32.7 us
  starting transfers between devices: 26 us -> 42.6 us
  between operations: 14.2 us -> 0.74 us
  blocking collectives: 12.7 us -> 0 us
  waiting for transfers between devices: 27.6 us -> 25.4 us
    pallas_call x4, Pallas kernels: 48.8 us -> 27.4 us  [the longest x1 15.9 us: prefill(): pl.pallas_call(functools.partial(prefill_kernel, tuple(segments)), out_sh...]
    ppermute x0 -> x8, starting transfers between devices: none -> 14.6 us  [along(): return lax.ppermute(array, 'z', [(i, (i + shift) % zs) for i in range(zs)])]
    all_to_all x1 -> x0, blocking collectives: 12.7 us -> none  [per_device(): lax.all_to_all(pack_kv(prefill_key, prefill_value), XY, 0, 0, tiled=True)]
    ppermute x0 -> x8, waiting for transfers between devices: none -> 12.1 us  [along(): return lax.ppermute(array, 'z', [(i, (i + shift) % zs) for i in range(zs)])]
    all_to_all x4 -> x5, waiting for transfers between devices: 21.1 us -> 13.3 us  [exchange(): return lax.all_to_all(array, axes, 0, 0, tiled=True)]
    all_gather x1 -> x0, waiting for transfers between devices: 6.49 us -> none  [per_device(): kv_all = lax.all_gather(kv, 'z', axis=0, tiled=False)]
    all_to_all x4 -> x5, starting transfers between devices: 25.9 us -> 28 us  [exchange(): return lax.all_to_all(array, axes, 0, 0, tiled=True)]
    unnamed x8 -> x10, local copies, waits for them, and re-layouts: 4.15 us -> 3.48 us
  transfers between devices with their start and end apart: 5 -> 13, of which waited for: 3 -> 5; matrix products, arithmetic and copies ran while one was open for 5% -> 7% of each run, Pallas kernels for 33% -> 26%
where the time goes in v2:
time: 113 us; the launch traced here: 112 us
  starting transfers between devices  42.6 us (38%)
  Pallas kernels  32.7 us (29%)
  waiting for transfers between devices  25.4 us (22%)
  local copies, waits for them, and re-layouts  6.3 us (6%)
  other arithmetic  4.5 us (4%)
    all_to_all x5, starting transfers between devices, exchange(): return lax.all_to_all(array, axes, 0, 0, tiled=True)  28 us
    pallas_call x1, Pallas kernels, prefill(): pl.pallas_call(functools.partial(prefill_kernel, tuple(segments)), out_sh...  15.9 us
    ppermute x8, starting transfers between devices, along(): return lax.ppermute(array, 'z', [(i, (i + shift) % zs) for i in range(zs)])  14.6 us
    all_to_all x5, waiting for transfers between devices, exchange(): return lax.all_to_all(array, axes, 0, 0, tiled=True)  13.3 us
    ppermute x8, waiting for transfers between devices, along(): return lax.ppermute(array, 'z', [(i, (i + shift) % zs) for i in range(zs)])  12.1 us
    pallas_call x1, Pallas kernels, verify(): pl.pallas_call(functools.partial(verify_kernel, tuple(segments)), out_sha...  6.92 us
    unnamed x10, local copies, waits for them, and re-layouts  3.48 us
    pallas_call x1, Pallas kernels, pack_q(): pl.pallas_call(pack_q_kernel, out_shape=jax.ShapeDtypeStruct((HK, q.shape...  2.26 us
  transfers between devices with their start and end apart: 13, of which 5 were waited for; matrix products, arithmetic and copies ran while one was open for 7% of the time, Pallas kernels for 26%

profile of v2, /device:TPU:32, one launch (start us, length us, event | category | flops | bytes accessed | tf_op | source)
XLA Modules:
  0.0 112.1 jit_solution(15529591902277155393)
XLA Ops:
  0.6 1.7 %pack_kv.1 = bf16[8,64,256]{2,1,0:T(8,128)(2,1)} custom-call(bf16[1,64,1024]{2,1,0:T(8,128)(2,1)} %k_ref.2, bf16[1,64,1024]{2,1,0:T(8,128)(2,1)} %v_ref.2), custom_call_target="tpu_custom_call" | custom-call | tf_op jit(solution)/shard_map/pack_kv/pallas_call | solution.py:318
  2.3 5.4 %all-to-all-start.1 = ((bf16[8,64,256]{2,1,0:T(8,128)(2,1)}), bf16[8,64,256]{2,1,0:T(8,128)(2,1)S(1)}, u32[]{:S(2)}, u32[]{:S(2)}) async-start(bf16[8,64,256]{2,1,0:T(8,128)(2,1)} %pack_kv.1), calls=%async_computation.1 | async-start | bytes 524288 | tf_op jit(solution)/shard_map/all_to_all | solution.py:445
  7.7 0.0 copy-start.1
  7.8 0.7 copy-done.1
  8.4 0.0 copy-start.2
  8.4 0.1 reshape.123
  8.6 0.5 copy-done.2
  9.1 0.1 reshape.124
  9.3 0.0 copy-start.4
  9.3 0.6 copy-done.4
  9.9 0.7 fusion.3
  10.6 0.7 fusion.2
  11.3 0.1 select_n.45
  11.4 1.8 %pack_rows.1 = bf16[32,8,1280]{2,1,0:T(8,128)(2,1)} custom-call(bf16[2,4,8192]{2,1,0:T(4,128)(2,1)} %q_ref.1, bf16[2,4,1024]{2,1,0:T(4,128)(2,1)} %k_ref.3, bf16[2,4,1024]{2,1,0:T(4,128)(2,1)} %v_ref.3), custom_call_target="tpu_custom_call" | custom-call | tf_op jit(solution)/shard_map/pack_rows/pallas_call | solution.py:370
  13.2 0.2 convert_reduce_fusion
  13.4 1.6 %all-to-all-done.1.refs_0_ = bf16[8,64,256]{2,1,0:T(8,128)(2,1)S(1)} async-done(((bf16[8,64,256]{2,1,0:T(8,128)(2,1)}), bf16[8,64,256]{2,1,0:T(8,128)(2,1)S(1)}, u32[]{:S(2)}, u32[]{:S(2)}) %all-to-all-start.1) | async-done | bytes 262176 | tf_op jit(solution)/shard_map/all_to_all | solution.py:445
  15.0 5.8 %all-to-all-start.3 = ((bf16[32,8,1280]{2,1,0:T(8,128)(2,1)}), bf16[32,8,1280]{2,1,0:T(8,128)(2,1)S(1)}, u32[]{:S(2)}, u32[]{:S(2)}) async-start(bf16[32,8,1280]{2,1,0:T(8,128)(2,1)} %pack_rows.1), calls=%async_computation.3 | async-start | bytes 1310720 | tf_op jit(solution)/shard_map/all_to_all | solution.py:445
  20.8 0.2 collective-permute-start.1
  21.0 1.9 %collective-permute-start = (bf16[8,64,256]{2,1,0:T(8,128)(2,1)S(1)}, bf16[8,64,256]{2,1,0:T(8,128)(2,1)S(1)}, u32[]{:S(2)}, u32[]{:S(2)}) collective-permute-start(bf16[8,64,256]{2,1,0:T(8,128)(2,1)S(1)} %all-to-all-done.1.refs_0_), channel_id=1, source_target_pairs={{0,1},{1,2},{2,3},{3,4},{4,5},{5,6},{6,7},{7,0},{8,9},{9,10},{10,1... | collective-permute-start | bytes 786440 | tf_op jit(solution)/shard_map/ppermute | solution.py:442
  22.9 6.6 %collective-permute-done.1.refs_2_ = bf16[8,64,256]{2,1,0:T(8,128)(2,1)S(1)} collective-permute-done((bf16[8,64,256]{2,1,0:T(8,128)(2,1)S(1)}, bf16[8,64,256]{2,1,0:T(8,128)(2,1)S(1)}, u32[]{:S(2)}, u32[]{:S(2)}) %collective-permute-start.1) | collective-permute-done | bytes 262176 | tf_op jit(solution)/shard_map/ppermute | solution.py:442
  29.5 3.3 %collective-permute-start.3 = (bf16[8,64,256]{2,1,0:T(8,128)(2,1)S(1)}, bf16[8,64,256]{2,1,0:T(8,128)(2,1)S(1)}, u32[]{:S(2)}, u32[]{:S(2)}) collective-permute-start(bf16[8,64,256]{2,1,0:T(8,128)(2,1)S(1)} %collective-permute-done.1.refs_2_), channel_id=1, source_target_pairs={{0,7},{1,0},{2,1},{3,2},{4,3},{5,4},{6,5},{7,6},{8,15},{9,8},{10,9... | collective-permute-start | bytes 786440 | tf_op jit(solution)/shard_map/ppermute | solution.py:442
  32.8 0.5 collective-permute-done.refs_1_
  33.3 0.0 collective-permute-start.2
  33.3 0.2 select_reduce_fusion
  33.5 2.3 %pack_q.1 = bf16[8,64,1024]{2,1,0:T(8,128)(2,1)} custom-call(bf16[1,64,8192]{2,1,0:T(8,128)(2,1)} %x_ref.1), custom_call_target="tpu_custom_call" | custom-call | tf_op jit(solution)/shard_map/pack_q/pallas_call | solution.py:331
  35.7 0.0 all-to-all-done.3.x_ref
  35.7 5.3 %all-to-all-start = ((bf16[8,64,1024]{2,1,0:T(8,128)(2,1)}), bf16[8,64,1024]{2,1,0:T(8,128)(2,1)S(1)}, u32[]{:S(2)}, u32[]{:S(2)}) async-start(bf16[8,64,1024]{2,1,0:T(8,128)(2,1)} %pack_q.1), calls=%async_computation | async-start | bytes 2097152 | tf_op jit(solution)/shard_map/all_to_all | solution.py:445
  41.1 0.7 broadcast_select_fusion
  41.7 0.0 collective-permute-done.3.refs_4_
  41.8 3.2 %collective-permute-start.5 = (bf16[8,64,256]{2,1,0:T(8,128)(2,1)S(1)}, bf16[8,64,256]{2,1,0:T(8,128)(2,1)S(1)}, u32[]{:S(2)}, u32[]{:S(2)}) collective-permute-start(bf16[8,64,256]{2,1,0:T(8,128)(2,1)S(1)} %collective-permute-done.3.refs_4_), channel_id=1, source_target_pairs={{0,7},{1,0},{2,1},{3,2},{4,3},{5,4},{6,5},{7,6},{8,15},{9,8},{10,9... | collective-permute-start | bytes 786440 | tf_op jit(solution)/shard_map/ppermute | solution.py:442
  45.0 0.0 collective-permute-done.2.refs_3_
  45.0 0.0 collective-permute-start.4
  45.0 0.7 fusion.4
  45.6 0.7 slice.9
  46.3 5.9 %collective-permute-start.7 = (bf16[8,32,256]{2,1,0:T(8,128)(2,1)}, bf16[8,32,256]{2,1,0:T(8,128)(2,1)S(1)}, u32[]{:S(2)}, u32[]{:S(2)}) collective-permute-start(bf16[8,32,256]{2,1,0:T(8,128)(2,1)} %slice.9), channel_id=1, source_target_pairs={{0,6},{1,7},{2,0},{3,1},{4,2},{5,3},{6,4},{7,5},{8,14},{9,15},{10,... | collective-permute-start | bytes 393224 | tf_op jit(solution)/shard_map/ppermute | solution.py:442
  52.2 0.7 slice.8
  52.9 0.0 collective-permute-start.6
  52.9 0.7 pad_add_fusion.1.info
  53.6 0.1 broadcast_in_dim.54
  53.7 0.1 convert_element_type.23.lim_row
  53.8 0.1 add.41.pos_row
  53.9 0.8 select_n.49.pos_col
  54.7 0.0 copy-start.3
  54.7 0.6 copy-done.3
  55.4 0.7 pad_add_fusion.info
  56.1 0.0 collective-permute-done.7.refs_8_
  56.1 5.0 %collective-permute-done.6.refs_7_ = bf16[8,32,256]{2,1,0:T(8,128)(2,1)} collective-permute-done((bf16[8,32,256]{2,1,0:T(8,128)(2,1)}, bf16[8,32,256]{2,1,0:T(8,128)(2,1)}, u32[]{:S(2)}, u32[]{:S(2)}) %collective-permute-start.6) | collective-permute-done | bytes 131104 | tf_op jit(solution)/shard_map/ppermute | solution.py:442
  61.1 0.0 collective-permute-done.5.refs_6_
  61.1 0.0 collective-permute-done.4.refs_5_
  61.1 6.9 %verify.1 = bf16[32,8,1024]{2,1,0:T(8,128)(2,1)} custom-call(s32[6]{0:T(128)S(1)} %pad_add_fusion.1.info, bf16[32,8,1280]{2,1,0:T(8,128)(2,1)S(1)} %all-to-all-done.3.x_ref, s32[1,256]{1,0:T(1,128)S(1)} %add.41.pos_row, f32[1,256]{1,0:T(1,128)S(1)} %convert_element_type.23.lim_row, s32[256,1]{1,0:T(8,128)S(1)} %select_n.49.pos_col, ...), custom_call_target="tpu_custom_call" | custom-call | flops 4000000000 | bytes 4194304 | tf_op jit(solution)/shard_map/verify/pallas_call | solution.py:283
  68.0 0.0 all-to-all-done.q_ref
  68.0 6.3 %all-to-all-start.4 = ((bf16[32,8,1024]{2,1,0:T(8,128)(2,1)}), bf16[32,8,1024]{2,1,0:T(8,128)(2,1)}, u32[]{:S(2)}, u32[]{:S(2)}) async-start(bf16[32,8,1024]{2,1,0:T(8,128)(2,1)} %verify.1), calls=%async_computation.4 | async-start | bytes 1048576 | tf_op jit(solution)/shard_map/all_to_all | solution.py:445
  74.3 15.9 %prefill.1 = bf16[8,64,1024]{2,1,0:T(8,128)(2,1)} custom-call(s32[62]{0:T(128)S(1)} %pad_add_fusion.info, bf16[8,64,1024]{2,1,0:T(8,128)(2,1)S(1)} %all-to-all-done.q_ref, bf16[8,64,256]{2,1,0:T(8,128)(2,1)S(1)} %all-to-all-done.1.refs_0_, bf16[8,64,256]{2,1,0:T(8,128)(2,1)S(1)} %collective-permute-done.refs_1_, ...), custom_call_target="tpu_custom_call" | custom-call | flops 20000000000 | bytes 4194304 | tf_op jit(solution)/shard_map/prefill/pallas_call | solution.py:181
  90.2 0.0 all-to-all-done.4.x_ref
  90.2 5.2 %all-to-all-start.2 = ((bf16[8,64,1024]{2,1,0:T(8,128)(2,1)}), bf16[8,64,1024]{2,1,0:T(8,128)(2,1)S(1)}, u32[]{:S(2)}, u32[]{:S(2)}) async-start(bf16[8,64,1024]{2,1,0:T(8,128)(2,1)} %prefill.1), calls=%async_computation.2 | async-start | bytes 2097152 | tf_op jit(solution)/shard_map/all_to_all | solution.py:445
  95.5 1.8 %sum_rows.1 = bf16[2,4,8192]{2,1,0:T(4,128)(2,1)} custom-call(bf16[32,8,1024]{2,1,0:T(8,128)(2,1)} %all-to-all-done.4.x_ref), custom_call_target="tpu_custom_call" | custom-call | tf_op jit(solution)/shard_map/sum_rows/pallas_call | solution.py:391
  97.2 11.7 %all-to-all-done.2.x_ref = bf16[8,64,1024]{2,1,0:T(8,128)(2,1)S(1)} async-done(((bf16[8,64,1024]{2,1,0:T(8,128)(2,1)}), bf16[8,64,1024]{2,1,0:T(8,128)(2,1)S(1)}, u32[]{:S(2)}, u32[]{:S(2)}) %all-to-all-start.2) | async-done | bytes 1048608 | tf_op jit(solution)/shard_map/all_to_all | solution.py:445
  108.9 0.0 copy-start
  108.9 1.0 copy-done
  109.9 2.3 %unpack_o.1 = bf16[1,64,8192]{2,1,0:T(8,128)(2,1)} custom-call(bf16[8,64,1024]{2,1,0:T(8,128)(2,1)} %copy-done), custom_call_target="tpu_custom_call" | custom-call | tf_op jit(solution)/shard_map/unpack_o/pallas_call | solution.py:344
  (4 shorter events, 0.0 us)
Async XLA Ops:
  2.3 12.6 %all-to-all-start.1 = ((bf16[8,64,256]{2,1,0:T(8,128)(2,1)}), bf16[8,64,256]{2,1,0:T(8,128)(2,1)S(1)}, u32[]{:S(2)}, u32[]{:S(2)}) async-start(bf16[8,64,256]{2,1,0:T(8,128)(2,1)} %pack_kv.1), calls=%async_computation.1 | async-start | bytes 524288 | tf_op jit(solution)/shard_map/all_to_all | solution.py:445
  7.7 0.7 copy-start.1
  8.4 0.7 copy-start.2
  9.3 0.7 copy-start.4
  15.0 20.8 %all-to-all-start.3 = ((bf16[32,8,1280]{2,1,0:T(8,128)(2,1)}), bf16[32,8,1280]{2,1,0:T(8,128)(2,1)S(1)}, u32[]{:S(2)}, u32[]{:S(2)}) async-start(bf16[32,8,1280]{2,1,0:T(8,128)(2,1)} %pack_rows.1), calls=%async_computation.3 | async-start | bytes 1310720 | tf_op jit(solution)/shard_map/all_to_all | solution.py:445
  20.8 8.7 %collective-permute-start.1 = (bf16[8,64,256]{2,1,0:T(8,128)(2,1)S(1)}, bf16[8,64,256]{2,1,0:T(8,128)(2,1)S(1)}, u32[]{:S(2)}, u32[]{:S(2)}) collective-permute-start(bf16[8,64,256]{2,1,0:T(8,128)(2,1)S(1)} %all-to-all-done.1.refs_0_), channel_id=1, source_target_pairs={{0,7},{1,0},{2,1},{3,2},{4,3},{5,4},{6,5},{7,6},{8,15},{9,8},{10,9... | collective-permute-start | bytes 786440 | tf_op jit(solution)/shard_map/ppermute | solution.py:442
  21.0 12.3 %collective-permute-start = (bf16[8,64,256]{2,1,0:T(8,128)(2,1)S(1)}, bf16[8,64,256]{2,1,0:T(8,128)(2,1)S(1)}, u32[]{:S(2)}, u32[]{:S(2)}) collective-permute-start(bf16[8,64,256]{2,1,0:T(8,128)(2,1)S(1)} %all-to-all-done.1.refs_0_), channel_id=1, source_target_pairs={{0,1},{1,2},{2,3},{3,4},{4,5},{5,6},{6,7},{7,0},{8,9},{9,10},{10,1... | collective-permute-start | bytes 786440 | tf_op jit(solution)/shard_map/ppermute | solution.py:442
  29.5 12.2 %collective-permute-start.3 = (bf16[8,64,256]{2,1,0:T(8,128)(2,1)S(1)}, bf16[8,64,256]{2,1,0:T(8,128)(2,1)S(1)}, u32[]{:S(2)}, u32[]{:S(2)}) collective-permute-start(bf16[8,64,256]{2,1,0:T(8,128)(2,1)S(1)} %collective-permute-done.1.refs_2_), channel_id=1, source_target_pairs={{0,7},{1,0},{2,1},{3,2},{4,3},{5,4},{6,5},{7,6},{8,15},{9,8},{10,9... | collective-permute-start | bytes 786440 | tf_op jit(solution)/shard_map/ppermute | solution.py:442
  33.3 11.7 %collective-permute-start.2 = (bf16[8,64,256]{2,1,0:T(8,128)(2,1)S(1)}, bf16[8,64,256]{2,1,0:T(8,128)(2,1)S(1)}, u32[]{:S(2)}, u32[]{:S(2)}) collective-permute-start(bf16[8,64,256]{2,1,0:T(8,128)(2,1)S(1)} %collective-permute-done.refs_1_), channel_id=1, source_target_pairs={{0,1},{1,2},{2,3},{3,4},{4,5},{5,6},{6,7},{7,0},{8,9},{9,10},{10,1... | collective-permute-start | bytes 786440 | tf_op jit(solution)/shard_map/ppermute | solution.py:442
  35.7 32.3 %all-to-all-start = ((bf16[8,64,1024]{2,1,0:T(8,128)(2,1)}), bf16[8,64,1024]{2,1,0:T(8,128)(2,1)S(1)}, u32[]{:S(2)}, u32[]{:S(2)}) async-start(bf16[8,64,1024]{2,1,0:T(8,128)(2,1)} %pack_q.1), calls=%async_computation | async-start | bytes 2097152 | tf_op jit(solution)/shard_map/all_to_all | solution.py:445
  41.8 19.4 %collective-permute-start.5 = (bf16[8,64,256]{2,1,0:T(8,128)(2,1)S(1)}, bf16[8,64,256]{2,1,0:T(8,128)(2,1)S(1)}, u32[]{:S(2)}, u32[]{:S(2)}) collective-permute-start(bf16[8,64,256]{2,1,0:T(8,128)(2,1)S(1)} %collective-permute-done.3.refs_4_), channel_id=1, source_target_pairs={{0,7},{1,0},{2,1},{3,2},{4,3},{5,4},{6,5},{7,6},{8,15},{9,8},{10,9... | collective-permute-start | bytes 786440 | tf_op jit(solution)/shard_map/ppermute | solution.py:442
  45.0 16.1 %collective-permute-start.4 = (bf16[8,64,256]{2,1,0:T(8,128)(2,1)S(1)}, bf16[8,64,256]{2,1,0:T(8,128)(2,1)}, u32[]{:S(2)}, u32[]{:S(2)}) collective-permute-start(bf16[8,64,256]{2,1,0:T(8,128)(2,1)S(1)} %collective-permute-done.2.refs_3_), channel_id=1, source_target_pairs={{0,1},{1,2},{2,3},{3,4},{4,5},{5,6},{6,7},{7,0},{8,9},{9,10},{10,1... | collective-permute-start | bytes 786440 | tf_op jit(solution)/shard_map/ppermute | solution.py:442
  46.3 9.8 %collective-permute-start.7 = (bf16[8,32,256]{2,1,0:T(8,128)(2,1)}, bf16[8,32,256]{2,1,0:T(8,128)(2,1)S(1)}, u32[]{:S(2)}, u32[]{:S(2)}) collective-permute-start(bf16[8,32,256]{2,1,0:T(8,128)(2,1)} %slice.9), channel_id=1, source_target_pairs={{0,6},{1,7},{2,0},{3,1},{4,2},{5,3},{6,4},{7,5},{8,14},{9,15},{10,... | collective-permute-start | bytes 393224 | tf_op jit(solution)/shard_map/ppermute | solution.py:442
  52.9 8.2 %collective-permute-start.6 = (bf16[8,32,256]{2,1,0:T(8,128)(2,1)}, bf16[8,32,256]{2,1,0:T(8,128)(2,1)}, u32[]{:S(2)}, u32[]{:S(2)}) collective-permute-start(bf16[8,32,256]{2,1,0:T(8,128)(2,1)} %slice.8), channel_id=1, source_target_pairs={{0,2},{1,3},{2,4},{3,5},{4,6},{5,7},{6,0},{7,1},{8,10},{9,11},{10,... | collective-permute-start | bytes 393224 | tf_op jit(solution)/shard_map/ppermute | solution.py:442
  54.7 0.7 copy-start.3
  68.0 22.2 %all-to-all-start.4 = ((bf16[32,8,1024]{2,1,0:T(8,128)(2,1)}), bf16[32,8,1024]{2,1,0:T(8,128)(2,1)}, u32[]{:S(2)}, u32[]{:S(2)}) async-start(bf16[32,8,1024]{2,1,0:T(8,128)(2,1)} %verify.1), calls=%async_computation.4 | async-start | bytes 1048576 | tf_op jit(solution)/shard_map/all_to_all | solution.py:445
  90.2 18.7 %all-to-all-start.2 = ((bf16[8,64,1024]{2,1,0:T(8,128)(2,1)}), bf16[8,64,1024]{2,1,0:T(8,128)(2,1)S(1)}, u32[]{:S(2)}, u32[]{:S(2)}) async-start(bf16[8,64,1024]{2,1,0:T(8,128)(2,1)} %prefill.1), calls=%async_computation.2 | async-start | bytes 2097152 | tf_op jit(solution)/shard_map/all_to_all | solution.py:445
  108.9 1.0 copy-start

commit v3 on v2

--- a/solution.py
+++ b/solution.py
@@ -14,6 +14,7 @@
 BLK = 64
 N_Z = 8
 STEPS = 4
+ROWS_DEV = 2
 BATCH = 16
 QH = HQ // HK
 HEAD_W = QH * HD
@@ -93,7 +94,7 @@
     kv_refs = refs[:n]
     o_ref, q_s, m_s, acc_s, sa, sb = refs[n:]
     z = info[0]
-    length = info[1]
+    length = info[2 + info[1]]
     count, tok, _ = q_ref.shape
     rows = QH * tok
     block = N_Z * tok
@@ -120,7 +121,10 @@
         m_s[p], acc_s[p] = softmax_step(s_ref[...], m_s[p], acc_s[p], v)
 
     def item(t):
-        return info[2 + 2 * t], info[3 + 2 * t]
+        starts = [j * (count - 1) - j * (j - 1) // 2 for j in range(1, count - 1)]
+        j = sum((t >= start).astype(jnp.int32) for start in starts)
+        p = jnp.minimum(t - j * (count - 1) + j * (j - 1) // 2 + j + 1, count - 1)
+        return p, j
 
     split(0)
     fill(sa, 0, 0)
@@ -139,7 +143,7 @@
     split(count - 1)
     fill(sb, count - 1, jnp.minimum(count - 1, edge))
     begin(sa, count - 2)
-    fill(sa, *item(0))
+    fill(sa, 1, 0)
     begin(sb, count - 1)
 
     def body(i, carry):
@@ -164,11 +168,6 @@
         return carry
 
     lax.fori_loop(0, count, finish, 0)
-
-
-def open_items(count):
-    pairs = [(p, j) for j in range(count - 1) for p in range(j + 1, count)] + [(1, 0)] * 2
-    return [k for pair in pairs for k in pair]
 
 
 def whole(shape):
@@ -194,7 +193,7 @@
                 pltpu.VMEM((rows, N_Z * tok), jnp.float32),
             ],
         ),
-        compiler_params=pltpu.CompilerParams(vmem_limit_bytes=40 * 2**20),
+        compiler_params=pltpu.CompilerParams(vmem_limit_bytes=24 * 2**20),
         cost_estimate=pl.CostEstimate(
             flops=20 * 10**9, transcendentals=10**7, bytes_accessed=4 * 2**20
         ),
@@ -202,21 +201,45 @@
     )(info, q, *kvs)
 
 
-def verify_kernel(segments, info, x_ref, pos_row, lim_row, pos_col, *refs):
+def across(column):
+    n = column.shape[0]
+    same = lax.broadcasted_iota(jnp.int32, (n, n), 0) == lax.broadcasted_iota(jnp.int32, (n, n), 1)
+    return jnp.sum(jnp.where(same, column, 0.0), axis=0, keepdims=True)
+
+
+def places_of_rows(z, g, length, cells, owner, cached):
+    total = owner.shape[1]
+    limit = jnp.where(owner == g, jnp.minimum(cached * BLK, length), 0).astype(jnp.float32)
+    cell = lax.broadcasted_iota(jnp.int32, (cells, 1), 0)
+    local = ROWS_DEV * STEPS
+    row = cell // local * (ROWS_DEV * N_Z) + z * ROWS_DEV + cell % local // STEPS
+    mine = lax.broadcasted_iota(jnp.int32, (cells, total), 1) == row
+    held = jnp.sum(jnp.where(mine, limit, 0.0), axis=1, keepdims=True)
+    other = across(held)
+    before = lax.broadcasted_iota(jnp.int32, (1, cells), 1) // STEPS < cell // STEPS
+    ahead = (other > held) | ((other == held) & before)
+    place = jnp.sum(jnp.where(ahead, 1.0, 0.0), axis=1, keepdims=True)
+    return held, place + (cell % STEPS).astype(jnp.float32)
+
+
+def verify_kernel(segments, info, x_ref, held_ref, *refs):
     n = len(segments)
     kv_refs = refs[:n]
     o_ref, x_s, lim_s, o_s, q_s, m_s, acc_s, sa, sb = refs[n:]
     z = info[0]
-    n_batch = info[1]
-    cells = pos_row.shape[1]
+    g = info[1]
+    length = info[2 + g]
+    cells = x_ref.shape[0] * x_ref.shape[1]
     blocks, tok, _ = kv_refs[0].shape
     width = N_Z * tok
     cut = BATCH * STEPS
     rows = QH * cut
-    pick = lax.broadcasted_iota(jnp.int32, (cells, cells), 0) == pos_row[...]
+    held, place_col = places_of_rows(z, g, length, cells, held_ref[0:1], held_ref[1:2])
+    index = lax.broadcasted_iota(jnp.int32, (cells, cells), 0).astype(jnp.float32)
+    pick = index == across(place_col)
     x = x_ref[...].reshape(cells, FRESH_W)
-    x_s[...] = dot_nn(pick.astype(jnp.bfloat16), x).astype(jnp.bfloat16)
-    limits = jnp.sum(jnp.where(pick, lim_row[...], 0.0), axis=1, keepdims=True)
+    x_s[...] = dot_nn(jnp.where(pick, 1.0, 0.0).astype(jnp.bfloat16), x).astype(jnp.bfloat16)
+    limits = jnp.sum(jnp.where(pick, across(held), 0.0), axis=1, keepdims=True)
     lim_s[...] = jnp.broadcast_to(limits, (cells, 128))
     o_s[...] = jnp.zeros((cells, HEAD_W), jnp.bfloat16)
     places = lane_groups(key_slots(segments, z, N_Z, tok, 1).astype(jnp.float32))
@@ -247,7 +270,8 @@
             v = joined_blocks(kv_refs, j, 1, VALUES)
             m_s[...], acc_s[...] = softmax_step(s, m_s[...], acc_s[...], v)
 
-        count = (info[2 + b] + width - 1) // width
+        most = jnp.max(lim_s[at, :]).astype(jnp.int32)
+        count = (most + width - 1) // width
         fill(sa, 0)
 
         def body(i, carry):
@@ -268,17 +292,19 @@
             o_s[at, h * HD : (h + 1) * HD] = out[h * cut : (h + 1) * cut, :]
         return carry
 
-    lax.fori_loop(0, n_batch, batch, 0)
-    place = lax.broadcasted_iota(jnp.int32, (cells, cells), 1) == pos_col[...]
-    out = dot_nn(place.astype(jnp.bfloat16), o_s[...]).astype(jnp.bfloat16)
+    owned = jnp.sum(jnp.where(held > 0.0, 1.0, 0.0)).astype(jnp.int32)
+    lax.fori_loop(0, (owned + cut - 1) // cut, batch, 0)
+    index = lax.broadcasted_iota(jnp.int32, (cells, cells), 1).astype(jnp.float32)
+    put = (index == place_col) & (held > 0.0)
+    out = dot_nn(jnp.where(put, 1.0, 0.0).astype(jnp.bfloat16), o_s[...]).astype(jnp.bfloat16)
     o_ref[...] = out.reshape(o_ref.shape)
 
 
-def verify(info, x, pos_row, lim_row, pos_col, kvs, segments):
-    cells = pos_row.shape[1]
+def verify(info, x, held, kvs, segments):
+    cells = x.shape[0] * x.shape[1]
     rows = QH * BATCH * STEPS
     width = N_Z * kvs[0].shape[1]
-    operands = (x, pos_row, lim_row, pos_col, *kvs)
+    operands = (x, held, *kvs)
     out = jax.ShapeDtypeStruct((*x.shape[:2], HEAD_W), x.dtype)
     return pl.pallas_call(
         functools.partial(verify_kernel, tuple(segments)),
@@ -299,7 +325,7 @@
                 pltpu.VMEM((rows, width), jnp.float32),
             ],
         ),
-        compiler_params=pltpu.CompilerParams(vmem_limit_bytes=40 * 2**20),
+        compiler_params=pltpu.CompilerParams(vmem_limit_bytes=24 * 2**20),
         cost_estimate=pl.CostEstimate(
             flops=4 * 10**9, transcendentals=10**6, bytes_accessed=4 * 2**20
         ),
@@ -331,6 +357,7 @@
     return pl.pallas_call(
         pack_q_kernel,
         out_shape=jax.ShapeDtypeStruct((HK, q.shape[1], HEAD_W), q.dtype),
+        compiler_params=pltpu.CompilerParams(vmem_limit_bytes=8 * 2**20),
         name="pack_q",
     )(q)
 
@@ -344,6 +371,7 @@
     return pl.pallas_call(
         unpack_o_kernel,
         out_shape=jax.ShapeDtypeStruct((1, o.shape[1], HK * HEAD_W), o.dtype),
+        compiler_params=pltpu.CompilerParams(vmem_limit_bytes=8 * 2**20),
         name="unpack_o",
     )(o)
 
@@ -370,6 +398,7 @@
     return pl.pallas_call(
         pack_rows_kernel,
         out_shape=jax.ShapeDtypeStruct((groups * HK, q.shape[0] * q.shape[1], FRESH_W), q.dtype),
+        compiler_params=pltpu.CompilerParams(vmem_limit_bytes=8 * 2**20),
         name="pack_rows",
     )(q, k, v)
 
@@ -391,30 +420,9 @@
     return pl.pallas_call(
         sum_rows_kernel,
         out_shape=jax.ShapeDtypeStruct((rows, steps, HK * HEAD_W), x.dtype),
+        compiler_params=pltpu.CompilerParams(vmem_limit_bytes=8 * 2**20),
         name="sum_rows",
     )(x)
-
-
-def tables(owner, cached, length, g, z, groups, per, zs, rows, steps):
-    own = lax.dynamic_index_in_dim(owner.reshape(groups, per, zs, rows), z, 2, False).reshape(-1)
-    held = lax.dynamic_index_in_dim(cached.reshape(groups, per, zs, rows), z, 2, False).reshape(-1)
-    limit = jnp.where(own == g, jnp.minimum(held * BLK, length), 0)
-    n = limit.shape[0]
-    index = jnp.arange(n, dtype=jnp.int32)
-    ahead = (limit[None, :] > limit[:, None]) | (
-        (limit[None, :] == limit[:, None]) & (index[None, :] < index[:, None])
-    )
-    rank = jnp.sum(ahead.astype(jnp.int32), axis=1)
-    pos = (rank[:, None] * steps + jnp.arange(steps, dtype=jnp.int32)[None, :]).reshape(-1)
-    mine = jnp.repeat(limit > 0, steps)
-    firsts = jnp.arange(n // BATCH, dtype=jnp.int32) * BATCH
-    tops = jnp.sum(jnp.where(rank[None, :] == firsts[:, None], limit[None, :], 0), axis=1)
-    n_batch = jnp.sum((tops > 0).astype(jnp.int32))
-    info = jnp.concatenate([z[None], n_batch[None], tops]).astype(jnp.int32)
-    pos_row = pos[None, :]
-    lim_row = jnp.repeat(limit, steps).astype(jnp.float32)[None, :]
-    pos_col = jnp.where(mine, pos, -1)[:, None]
-    return info, pos_row, lim_row, pos_col
 
 
 def per_device(
@@ -430,13 +438,11 @@
 ):
     groups = lax.axis_size("g")
     zs = lax.axis_size("z")
-    per = lax.axis_size(XY)
     g = lax.axis_index("g")
     z = lax.axis_index("z")
     rows, steps, _ = verify_query.shape
     tok = prefill_query.shape[1]
     half = tok // 2
-    length = jnp.sum(jnp.where(jnp.arange(groups, dtype=jnp.int32) == g, lengths, 0))
 
     def along(array, shift):
         return lax.ppermute(array, "z", [(i, (i + shift) % zs) for i in range(zs)])
@@ -447,27 +453,23 @@
     own = exchange(pack_kv(prefill_key, prefill_value), XY)
     q_in = pack_q(prefill_query)
     x_in = pack_rows(verify_query, verify_key, verify_value, groups)
+    up1, down1 = along(own, 1), along(own, -1)
     q = exchange(q_in, XY)
-    up1, down1 = along(own, 1), along(own, -1)
+    up2, down2 = along(up1, 1), along(down1, -1)
+    up4 = along(up1[:, :half], 3)
+    down4 = along(down1[:, half:], -3)
+    up3, down3 = along(up2, 1), along(down2, -1)
     x = exchange(x_in, GXY)
-    up2, down2 = along(up1, 1), along(down1, -1)
-    up3, down3 = along(up2, 1), along(down2, -1)
-    up4 = along(up2[:, :half], 2)
-    down4 = along(down2[:, half:], -2)
     kvs = [own, up1, down1, up2, down2, up3, down3, up4, down4]
     segments = [(s, 0, tok) for s in (0, 1, -1, 2, -2, 3, -3)]
     segments += [(4, 0, half), (4, half, half)]
 
-    where = jnp.concatenate(
-        [jnp.stack([z, length]), jnp.array(open_items(per), dtype=jnp.int32)]
-    ).astype(jnp.int32)
-    info, pos_row, lim_row, pos_col = tables(
-        owner, cached, length, g, z, groups, per, zs, rows, steps
-    )
-    decoded = verify(info, x, pos_row, lim_row, pos_col, kvs, segments)
+    info = jnp.concatenate([jnp.stack([z, g]), lengths]).astype(jnp.int32)
+    held = jnp.stack([owner, cached])
+    out = prefill(info, q, kvs, segments)
+    out = exchange(out, XY)
+    decoded = verify(info, x, held, kvs, segments)
     returned = exchange(decoded, GXY)
-    out = prefill(where, q, kvs, segments)
-    out = exchange(out, XY)
     return unpack_o(out), sum_rows(returned, rows, steps)
 
 

time: 113 us -> 117 us (1.035)
  the two profiles are of different devices: /device:TPU:32 before, /device:TPU:2 now
where the time goes in v3:
time: 117 us; the launch traced here: 116 us
  starting transfers between devices  48.4 us (41%)
  waiting for transfers between devices  36.7 us (31%)
  Pallas kernels  26.8 us (23%)
  local copies, waits for them, and re-layouts  3.59 us (3%)
    all_to_all x5, starting transfers between devices, exchange(): return lax.all_to_all(array, axes, 0, 0, tiled=True)  28.9 us
    all_to_all x5, waiting for transfers between devices, exchange(): return lax.all_to_all(array, axes, 0, 0, tiled=True)  21.3 us
    ppermute x8, starting transfers between devices, along(): return lax.ppermute(array, 'z', [(i, (i + shift) % zs) for i in range(zs)])  19.5 us
    ppermute x8, waiting for transfers between devices, along(): return lax.ppermute(array, 'z', [(i, (i + shift) % zs) for i in range(zs)])  15.4 us
    pallas_call x1, Pallas kernels, prefill(): pl.pallas_call(functools.partial(prefill_kernel, tuple(segments)), out_sh...  15.1 us
    pallas_call x1, Pallas kernels, verify(): pl.pallas_call(functools.partial(verify_kernel, tuple(segments)), out_sha...  6.24 us
    unnamed x22, local copies, waits for them, and re-layouts  3.57 us
  transfers between devices with their start and end apart: 13, of which 7 were waited for; matrix products, arithmetic and copies ran while one was open for 0% of the time, Pallas kernels for 21%

profile of v3, /device:TPU:2, one launch (start us, length us, event | category | flops | bytes accessed | tf_op | source)
XLA Modules:
  0.0 116.2 jit_solution(12267035865697659368)
XLA Ops:
  0.6 1.7 %pack_kv.1 = bf16[8,64,256]{2,1,0:T(8,128)(2,1)} custom-call(bf16[1,64,1024]{2,1,0:T(8,128)(2,1)} %k_ref.2, bf16[1,64,1024]{2,1,0:T(8,128)(2,1)} %v_ref.2), custom_call_target="tpu_custom_call" | custom-call | tf_op jit(solution)/shard_map/pack_kv/pallas_call | solution.py:344
  2.3 0.0 copy-start.1
  2.3 0.0 copy-start.2
  2.4 0.0 copy-start.3
  2.4 6.1 %all-to-all-start.1 = ((bf16[8,64,256]{2,1,0:T(8,128)(2,1)}), bf16[8,64,256]{2,1,0:T(8,128)(2,1)S(1)}, u32[]{:S(2)}, u32[]{:S(2)}) async-start(bf16[8,64,256]{2,1,0:T(8,128)(2,1)} %pack_kv.1), calls=%async_computation.1 | async-start | bytes 524288 | tf_op jit(solution)/shard_map/all_to_all | solution.py:451
  8.4 0.0 copy-done.1
  8.4 0.0 copy-done.2
  8.4 0.0 copy-done.3
  8.4 0.0 copy-start
  8.4 0.9 pack_rows.1
  9.3 4.9 %all-to-all-done.1.refs_0_ = bf16[8,64,256]{2,1,0:T(8,128)(2,1)S(1)} async-done(((bf16[8,64,256]{2,1,0:T(8,128)(2,1)}), bf16[8,64,256]{2,1,0:T(8,128)(2,1)S(1)}, u32[]{:S(2)}, u32[]{:S(2)}) %all-to-all-start.1) | async-done | bytes 262176 | tf_op jit(solution)/shard_map/all_to_all | solution.py:451
  14.2 5.9 %all-to-all-start.3 = ((bf16[32,8,1280]{2,1,0:T(8,128)(2,1)}), bf16[32,8,1280]{2,1,0:T(8,128)(2,1)S(1)}, u32[]{:S(2)}, u32[]{:S(2)}) async-start(bf16[32,8,1280]{2,1,0:T(8,128)(2,1)} %pack_rows.1), calls=%async_computation.3 | async-start | bytes 1310720 | tf_op jit(solution)/shard_map/all_to_all | solution.py:451
  20.2 5.9 %collective-permute-start.1 = (bf16[8,64,256]{2,1,0:T(8,128)(2,1)S(1)}, bf16[8,64,256]{2,1,0:T(8,128)(2,1)S(1)}, u32[]{:S(2)}, u32[]{:S(2)}) collective-permute-start(bf16[8,64,256]{2,1,0:T(8,128)(2,1)S(1)} %all-to-all-done.1.refs_0_), channel_id=1, source_target_pairs={{0,7},{1,0},{2,1},{3,2},{4,3},{5,4},{6,5},{7,6},{8,15},{9,8},{10,9... | collective-permute-start | bytes 786440 | tf_op jit(solution)/shard_map/ppermute | solution.py:448
  26.1 0.0 collective-permute-start
  26.1 0.0 copy-done
  26.1 1.0 pack_q.1
  27.1 4.2 %all-to-all-done.3.x_ref = bf16[32,8,1280]{2,1,0:T(8,128)(2,1)S(1)} async-done(((bf16[32,8,1280]{2,1,0:T(8,128)(2,1)}), bf16[32,8,1280]{2,1,0:T(8,128)(2,1)S(1)}, u32[]{:S(2)}, u32[]{:S(2)}) %all-to-all-start.3) | async-done | bytes 655392 | tf_op jit(solution)/shard_map/all_to_all | solution.py:451
  31.4 5.2 %all-to-all-start = ((bf16[8,64,1024]{2,1,0:T(8,128)(2,1)}), bf16[8,64,1024]{2,1,0:T(8,128)(2,1)S(1)}, u32[]{:S(2)}, u32[]{:S(2)}) async-start(bf16[8,64,1024]{2,1,0:T(8,128)(2,1)} %pack_q.1), calls=%async_computation | async-start | bytes 2097152 | tf_op jit(solution)/shard_map/all_to_all | solution.py:451
  36.6 0.0 collective-permute-done.1.refs_2_
  36.6 5.9 %collective-permute-start.3 = (bf16[8,64,256]{2,1,0:T(8,128)(2,1)S(1)}, bf16[8,64,256]{2,1,0:T(8,128)(2,1)S(1)}, u32[]{:S(2)}, u32[]{:S(2)}) collective-permute-start(bf16[8,64,256]{2,1,0:T(8,128)(2,1)S(1)} %collective-permute-done.1.refs_2_), channel_id=1, source_target_pairs={{0,7},{1,0},{2,1},{3,2},{4,3},{5,4},{6,5},{7,6},{8,15},{9,8},{10,9... | collective-permute-start | bytes 786440 | tf_op jit(solution)/shard_map/ppermute | solution.py:448
  42.5 0.0 collective-permute-done.refs_1_
  42.5 0.0 collective-permute-start.2
  42.5 5.6 %collective-permute-done.3.refs_4_ = bf16[8,64,256]{2,1,0:T(8,128)(2,1)S(1)} collective-permute-done((bf16[8,64,256]{2,1,0:T(8,128)(2,1)S(1)}, bf16[8,64,256]{2,1,0:T(8,128)(2,1)S(1)}, u32[]{:S(2)}, u32[]{:S(2)}) %collective-permute-start.3) | collective-permute-done | bytes 262176 | tf_op jit(solution)/shard_map/ppermute | solution.py:448
  48.1 3.7 %collective-permute-start.5 = (bf16[8,64,256]{2,1,0:T(8,128)(2,1)S(1)}, bf16[8,64,256]{2,1,0:T(8,128)(2,1)S(1)}, u32[]{:S(2)}, u32[]{:S(2)}) collective-permute-start(bf16[8,64,256]{2,1,0:T(8,128)(2,1)S(1)} %collective-permute-done.3.refs_4_), channel_id=1, source_target_pairs={{0,7},{1,0},{2,1},{3,2},{4,3},{5,4},{6,5},{7,6},{8,15},{9,8},{10,9... | collective-permute-start | bytes 786440 | tf_op jit(solution)/shard_map/ppermute | solution.py:448
  51.8 0.0 collective-permute-done.2.refs_3_
  51.8 0.0 collective-permute-start.4
  51.8 1.8 %collective-permute-start.7 = (bf16[8,32,256]{2,1,0:T(8,128)(2,1)S(1)}, bf16[8,32,256]{2,1,0:T(8,128)(2,1)S(1)}, u32[]{:S(2)}, u32[]{:S(2)}) collective-permute-start(bf16[8,32,256]{2,1,0:T(8,128)(2,1)S(1)} %slice.9), channel_id=1, source_target_pairs={{0,5},{1,6},{2,7},{3,0},{4,1},{5,2},{6,3},{7,4},{8,13},{9,14},{10,... | collective-permute-start | bytes 393224 | tf_op jit(solution)/shard_map/ppermute | solution.py:448
  53.6 2.2 %collective-permute-start.6 = (bf16[8,32,256]{2,1,0:T(8,128)(2,1)S(1)}, bf16[8,32,256]{2,1,0:T(8,128)(2,1)S(1)}, u32[]{:S(2)}, u32[]{:S(2)}) collective-permute-start(bf16[8,32,256]{2,1,0:T(8,128)(2,1)S(1)} %slice.8), channel_id=1, source_target_pairs={{0,3},{1,4},{2,5},{3,6},{4,7},{5,0},{6,1},{7,2},{8,11},{9,12},{10,... | collective-permute-start | bytes 393224 | tf_op jit(solution)/shard_map/ppermute | solution.py:448
  55.8 0.0 copy-start.10
  55.8 0.7 copy-done.10
  56.5 0.0 copy-start.9
  56.5 0.1 pad_add_fusion.1.info
  56.6 0.0 copy-start.8
  56.6 0.6 copy-done.9
  57.2 0.1 copy-done.8
  57.3 7.8 %collective-permute-done.7.refs_8_ = bf16[8,32,256]{2,1,0:T(8,128)(2,1)S(1)} collective-permute-done((bf16[8,32,256]{2,1,0:T(8,128)(2,1)S(1)}, bf16[8,32,256]{2,1,0:T(8,128)(2,1)S(1)}, u32[]{:S(2)}, u32[]{:S(2)}) %collective-permute-start.7) | collective-permute-done | bytes 131104 | tf_op jit(solution)/shard_map/ppermute | solution.py:448
  65.0 0.2 collective-permute-done.6.refs_7_
  65.2 0.0 collective-permute-done.5.refs_6_
  65.2 1.8 %collective-permute-done.4.refs_5_ = bf16[8,64,256]{2,1,0:T(8,128)(2,1)S(1)} collective-permute-done((bf16[8,64,256]{2,1,0:T(8,128)(2,1)S(1)}, bf16[8,64,256]{2,1,0:T(8,128)(2,1)S(1)}, u32[]{:S(2)}, u32[]{:S(2)}) %collective-permute-start.4) | collective-permute-done | bytes 262176 | tf_op jit(solution)/shard_map/ppermute | solution.py:448
  67.0 6.2 %verify.1 = bf16[32,8,1024]{2,1,0:T(8,128)(2,1)} custom-call(s32[6]{0:T(128)S(1)} %pad_add_fusion.1.info, bf16[32,8,1280]{2,1,0:T(8,128)(2,1)S(1)} %all-to-all-done.3.x_ref, s32[2,512]{1,0:T(2,128)S(1)} %pad_add_fusion.held_ref, bf16[8,64,256]{2,1,0:T(8,128)(2,1)S(1)} %all-to-all-done.1.refs_0_, bf16[8,64,256]{2,1,0:T(8,128)(2,1)S(1)} %collective-permute-done.refs_1_, ...), custom_call_target="tpu_custom_call" | custom-call | flops 4000000000 | bytes 4194304 | tf_op jit(solution)/shard_map/verify/pallas_call | solution.py:309
  73.3 0.0 copy-start.4
  73.3 0.7 copy-done.4
  73.9 0.0 copy-start.6
  73.9 0.7 copy-done.6
  74.6 0.0 all-to-all-done.q_ref
  74.6 0.0 copy-start.5
  74.6 6.0 %all-to-all-start.4 = ((bf16[32,8,1024]{2,1,0:T(8,128)(2,1)}), bf16[32,8,1024]{2,1,0:T(8,128)(2,1)S(1)}, u32[]{:S(2)}, u32[]{:S(2)}) async-start(bf16[32,8,1024]{2,1,0:T(8,128)(2,1)} %verify.1), calls=%async_computation.4 | async-start | bytes 1048576 | tf_op jit(solution)/shard_map/all_to_all | solution.py:451
  80.6 0.0 copy-done.5
  80.6 0.0 copy-start.7
  80.6 0.9 copy-done.7
  81.5 15.1 %prefill.1 = bf16[8,64,1024]{2,1,0:T(8,128)(2,1)} custom-call(s32[6]{0:T(128)S(1)} %pad_add_fusion.1.info, bf16[8,64,1024]{2,1,0:T(8,128)(2,1)S(1)} %all-to-all-done.q_ref, bf16[8,64,256]{2,1,0:T(8,128)(2,1)S(1)} %all-to-all-done.1.refs_0_, bf16[8,64,256]{2,1,0:T(8,128)(2,1)S(1)} %collective-permute-done.refs_1_, ...), custom_call_target="tpu_custom_call" | custom-call | flops 20000000000 | bytes 4194304 | tf_op jit(solution)/shard_map/prefill/pallas_call | solution.py:180
  96.6 0.0 all-to-all-done.4.x_ref
  96.6 5.7 %all-to-all-start.2 = ((bf16[8,64,1024]{2,1,0:T(8,128)(2,1)}), bf16[8,64,1024]{2,1,0:T(8,128)(2,1)S(1)}, u32[]{:S(2)}, u32[]{:S(2)}) async-start(bf16[8,64,1024]{2,1,0:T(8,128)(2,1)} %prefill.1), calls=%async_computation.2 | async-start | bytes 2097152 | tf_op jit(solution)/shard_map/all_to_all | solution.py:451
  102.3 0.7 sum_rows.1
  103.1 12.1 %all-to-all-done.2.x_ref = bf16[8,64,1024]{2,1,0:T(8,128)(2,1)S(1)} async-done(((bf16[8,64,1024]{2,1,0:T(8,128)(2,1)}), bf16[8,64,1024]{2,1,0:T(8,128)(2,1)S(1)}, u32[]{:S(2)}, u32[]{:S(2)}) %all-to-all-start.2) | async-done | bytes 1048608 | tf_op jit(solution)/shard_map/all_to_all | solution.py:451
  115.2 1.0 unpack_o.1
  (3 shorter events, 0.0 us)
Async XLA Ops:
  2.3 6.1 %copy-start.1 = (bf16[2,4,8192]{2,1,0:T(4,128)(2,1)S(1)}, bf16[2,4,8192]{2,1,0:T(4,128)(2,1)}, u32[]{:S(2)}) copy-start(bf16[2,4,8192]{2,1,0:T(4,128)(2,1)} %q_ref.1) | copy-start | bytes 393220
  2.3 6.1 %copy-start.2 = (bf16[2,4,1024]{2,1,0:T(4,128)(2,1)S(1)}, bf16[2,4,1024]{2,1,0:T(4,128)(2,1)}, u32[]{:S(2)}) copy-start(bf16[2,4,1024]{2,1,0:T(4,128)(2,1)} %k_ref.3) | copy-start | bytes 49156
  2.4 6.1 %copy-start.3 = (bf16[2,4,1024]{2,1,0:T(4,128)(2,1)S(1)}, bf16[2,4,1024]{2,1,0:T(4,128)(2,1)}, u32[]{:S(2)}) copy-start(bf16[2,4,1024]{2,1,0:T(4,128)(2,1)} %v_ref.3) | copy-start | bytes 49156
  2.4 11.9 %all-to-all-start.1 = ((bf16[8,64,256]{2,1,0:T(8,128)(2,1)}), bf16[8,64,256]{2,1,0:T(8,128)(2,1)S(1)}, u32[]{:S(2)}, u32[]{:S(2)}) async-start(bf16[8,64,256]{2,1,0:T(8,128)(2,1)} %pack_kv.1), calls=%async_computation.1 | async-start | bytes 524288 | tf_op jit(solution)/shard_map/all_to_all | solution.py:451
  8.4 17.7 %copy-start = (bf16[1,64,8192]{2,1,0:T(8,128)(2,1)S(1)}, bf16[1,64,8192]{2,1,0:T(8,128)(2,1)}, u32[]{:S(2)}) copy-start(bf16[1,64,8192]{2,1,0:T(8,128)(2,1)} %x_ref.1) | copy-start | bytes 3145732
  14.2 17.1 %all-to-all-start.3 = ((bf16[32,8,1280]{2,1,0:T(8,128)(2,1)}), bf16[32,8,1280]{2,1,0:T(8,128)(2,1)S(1)}, u32[]{:S(2)}, u32[]{:S(2)}) async-start(bf16[32,8,1280]{2,1,0:T(8,128)(2,1)} %pack_rows.1), calls=%async_computation.3 | async-start | bytes 1310720 | tf_op jit(solution)/shard_map/all_to_all | solution.py:451
  20.2 16.5 %collective-permute-start.1 = (bf16[8,64,256]{2,1,0:T(8,128)(2,1)S(1)}, bf16[8,64,256]{2,1,0:T(8,128)(2,1)S(1)}, u32[]{:S(2)}, u32[]{:S(2)}) collective-permute-start(bf16[8,64,256]{2,1,0:T(8,128)(2,1)S(1)} %all-to-all-done.1.refs_0_), channel_id=1, source_target_pairs={{0,7},{1,0},{2,1},{3,2},{4,3},{5,4},{6,5},{7,6},{8,15},{9,8},{10,9... | collective-permute-start | bytes 786440 | tf_op jit(solution)/shard_map/ppermute | solution.py:448
  26.1 16.4 %collective-permute-start = (bf16[8,64,256]{2,1,0:T(8,128)(2,1)S(1)}, bf16[8,64,256]{2,1,0:T(8,128)(2,1)S(1)}, u32[]{:S(2)}, u32[]{:S(2)}) collective-permute-start(bf16[8,64,256]{2,1,0:T(8,128)(2,1)S(1)} %all-to-all-done.1.refs_0_), channel_id=1, source_target_pairs={{0,1},{1,2},{2,3},{3,4},{4,5},{5,6},{6,7},{7,0},{8,9},{9,10},{10,1... | collective-permute-start | bytes 786440 | tf_op jit(solution)/shard_map/ppermute | solution.py:448
  31.4 43.2 %all-to-all-start = ((bf16[8,64,1024]{2,1,0:T(8,128)(2,1)}), bf16[8,64,1024]{2,1,0:T(8,128)(2,1)S(1)}, u32[]{:S(2)}, u32[]{:S(2)}) async-start(bf16[8,64,1024]{2,1,0:T(8,128)(2,1)} %pack_q.1), calls=%async_computation | async-start | bytes 2097152 | tf_op jit(solution)/shard_map/all_to_all | solution.py:451
  36.6 11.5 %collective-permute-start.3 = (bf16[8,64,256]{2,1,0:T(8,128)(2,1)S(1)}, bf16[8,64,256]{2,1,0:T(8,128)(2,1)S(1)}, u32[]{:S(2)}, u32[]{:S(2)}) collective-permute-start(bf16[8,64,256]{2,1,0:T(8,128)(2,1)S(1)} %collective-permute-done.1.refs_2_), channel_id=1, source_target_pairs={{0,7},{1,0},{2,1},{3,2},{4,3},{5,4},{6,5},{7,6},{8,15},{9,8},{10,9... | collective-permute-start | bytes 786440 | tf_op jit(solution)/shard_map/ppermute | solution.py:448
  42.5 9.3 %collective-permute-start.2 = (bf16[8,64,256]{2,1,0:T(8,128)(2,1)S(1)}, bf16[8,64,256]{2,1,0:T(8,128)(2,1)S(1)}, u32[]{:S(2)}, u32[]{:S(2)}) collective-permute-start(bf16[8,64,256]{2,1,0:T(8,128)(2,1)S(1)} %collective-permute-done.refs_1_), channel_id=1, source_target_pairs={{0,1},{1,2},{2,3},{3,4},{4,5},{5,6},{6,7},{7,0},{8,9},{9,10},{10,1... | collective-permute-start | bytes 786440 | tf_op jit(solution)/shard_map/ppermute | solution.py:448
  48.1 17.1 %collective-permute-start.5 = (bf16[8,64,256]{2,1,0:T(8,128)(2,1)S(1)}, bf16[8,64,256]{2,1,0:T(8,128)(2,1)S(1)}, u32[]{:S(2)}, u32[]{:S(2)}) collective-permute-start(bf16[8,64,256]{2,1,0:T(8,128)(2,1)S(1)} %collective-permute-done.3.refs_4_), channel_id=1, source_target_pairs={{0,7},{1,0},{2,1},{3,2},{4,3},{5,4},{6,5},{7,6},{8,15},{9,8},{10,9... | collective-permute-start | bytes 786440 | tf_op jit(solution)/shard_map/ppermute | solution.py:448
  51.8 15.2 %collective-permute-start.4 = (bf16[8,64,256]{2,1,0:T(8,128)(2,1)S(1)}, bf16[8,64,256]{2,1,0:T(8,128)(2,1)S(1)}, u32[]{:S(2)}, u32[]{:S(2)}) collective-permute-start(bf16[8,64,256]{2,1,0:T(8,128)(2,1)S(1)} %collective-permute-done.2.refs_3_), channel_id=1, source_target_pairs={{0,1},{1,2},{2,3},{3,4},{4,5},{5,6},{6,7},{7,0},{8,9},{9,10},{10,1... | collective-permute-start | bytes 786440 | tf_op jit(solution)/shard_map/ppermute | solution.py:448
  51.8 13.2 %collective-permute-start.7 = (bf16[8,32,256]{2,1,0:T(8,128)(2,1)S(1)}, bf16[8,32,256]{2,1,0:T(8,128)(2,1)S(1)}, u32[]{:S(2)}, u32[]{:S(2)}) collective-permute-start(bf16[8,32,256]{2,1,0:T(8,128)(2,1)S(1)} %slice.9), channel_id=1, source_target_pairs={{0,5},{1,6},{2,7},{3,0},{4,1},{5,2},{6,3},{7,4},{8,13},{9,14},{10,... | collective-permute-start | bytes 393224 | tf_op jit(solution)/shard_map/ppermute | solution.py:448
  53.6 11.6 %collective-permute-start.6 = (bf16[8,32,256]{2,1,0:T(8,128)(2,1)S(1)}, bf16[8,32,256]{2,1,0:T(8,128)(2,1)S(1)}, u32[]{:S(2)}, u32[]{:S(2)}) collective-permute-start(bf16[8,32,256]{2,1,0:T(8,128)(2,1)S(1)} %slice.8), channel_id=1, source_target_pairs={{0,3},{1,4},{2,5},{3,6},{4,7},{5,0},{6,1},{7,2},{8,11},{9,12},{10,... | collective-permute-start | bytes 393224 | tf_op jit(solution)/shard_map/ppermute | solution.py:448
  55.8 0.7 copy-start.10
  56.5 0.7 copy-start.9
  56.6 0.7 copy-start.8
  73.3 0.7 copy-start.4
  73.9 0.7 copy-start.6
  74.6 6.0 %copy-start.5 = (bf16[8,32,256]{2,1,0:T(8,128)(2,1)S(1)}, bf16[8,32,256]{2,1,0:T(8,128)(2,1)}, u32[]{:S(2)}) copy-start(bf16[8,32,256]{2,1,0:T(8,128)(2,1)} %copy-done.4) | copy-start | bytes 393220
  74.6 22.1 %all-to-all-start.4 = ((bf16[32,8,1024]{2,1,0:T(8,128)(2,1)}), bf16[32,8,1024]{2,1,0:T(8,128)(2,1)S(1)}, u32[]{:S(2)}, u32[]{:S(2)}) async-start(bf16[32,8,1024]{2,1,0:T(8,128)(2,1)} %verify.1), calls=%async_computation.4 | async-start | bytes 1048576 | tf_op jit(solution)/shard_map/all_to_all | solution.py:451
  80.6 0.9 copy-start.7
  96.6 18.5 %all-to-all-start.2 = ((bf16[8,64,1024]{2,1,0:T(8,128)(2,1)}), bf16[8,64,1024]{2,1,0:T(8,128)(2,1)S(1)}, u32[]{:S(2)}, u32[]{:S(2)}) async-start(bf16[8,64,1024]{2,1,0:T(8,128)(2,1)} %prefill.1), calls=%async_computation.2 | async-start | bytes 2097152 | tf_op jit(solution)/shard_map/all_to_all | solution.py:451

commit v4 on v3

--- a/solution.py
+++ b/solution.py
@@ -129,33 +129,37 @@
     split(0)
     fill(sa, 0, 0)
 
-    def edges(i, carry):
-        p = 2 * i
+    for p in range(0, count - 2, 2):
         split(p + 1)
         fill(sb, p + 1, jnp.minimum(p + 1, edge))
         begin(sa, p)
         split(p + 2)
         fill(sa, p + 2, jnp.minimum(p + 2, edge))
         begin(sb, p + 1)
-        return carry
-
-    lax.fori_loop(0, count // 2 - 1, edges, 0)
     split(count - 1)
     fill(sb, count - 1, jnp.minimum(count - 1, edge))
     begin(sa, count - 2)
     fill(sa, 1, 0)
     begin(sb, count - 1)
 
+    def two(t):
+        fill(sb, *item(t + 1))
+        take(sa, *item(t))
+        fill(sa, *item(t + 2))
+        take(sb, *item(t + 1))
+
     def body(i, carry):
-        fill(sb, *item(2 * i + 1))
-        take(sa, *item(2 * i))
-        fill(sa, *item(2 * i + 2))
-        take(sb, *item(2 * i + 1))
+        two(4 * i)
+        two(4 * i + 2)
         return carry
 
     cols = jnp.minimum(edge, count - 1)
     items = (count - 1) * cols - cols * (cols - 1) // 2
-    lax.fori_loop(0, items // 2, body, 0)
+    lax.fori_loop(0, items // 4, body, 0)
+
+    @pl.when(items % 4 >= 2)
+    def _():
+        two(items // 4 * 4)
 
     @pl.when(items % 2 == 1)
     def _():
@@ -222,25 +226,53 @@
     return held, place + (cell % STEPS).astype(jnp.float32)
 
 
-def verify_kernel(segments, info, x_ref, held_ref, *refs):
+def sort_kernel(info, x_ref, held_ref, x_out, lim_out, place_out):
+    g = info[1]
+    cells = x_ref.shape[0] * x_ref.shape[1]
+    held, place_col = places_of_rows(
+        info[0], g, info[2 + g], cells, held_ref[0:1], held_ref[1:2]
+    )
+    index = lax.broadcasted_iota(jnp.int32, (cells, cells), 0).astype(jnp.float32)
+    pick = index == across(place_col)
+    x = x_ref[...].reshape(cells, FRESH_W)
+    x_out[...] = dot_nn(jnp.where(pick, 1.0, 0.0).astype(jnp.bfloat16), x).astype(jnp.bfloat16)
+    limits = jnp.sum(jnp.where(pick, across(held), 0.0), axis=1, keepdims=True)
+    lim_out[...] = jnp.broadcast_to(limits, (cells, 128))
+    place = jnp.where(held > 0.0, place_col, -1.0)
+    place_out[...] = jnp.broadcast_to(place, (cells, 128))
+
+
+def sort_rows(info, x, held):
+    cells = x.shape[0] * x.shape[1]
+    outs = (
+        jax.ShapeDtypeStruct((cells, FRESH_W), x.dtype),
+        jax.ShapeDtypeStruct((cells, 128), jnp.float32),
+        jax.ShapeDtypeStruct((cells, 128), jnp.float32),
+    )
+    return pl.pallas_call(
+        sort_kernel,
+        out_shape=outs,
+        grid_spec=pltpu.PrefetchScalarGridSpec(
+            num_scalar_prefetch=1,
+            grid=(1,),
+            in_specs=[whole(a.shape) for a in (x, held)],
+            out_specs=tuple(whole(a.shape) for a in outs),
+        ),
+        compiler_params=pltpu.CompilerParams(vmem_limit_bytes=16 * 2**20),
+        name="sort_rows",
+    )(info, x, held)
+
+
+def verify_kernel(segments, info, x_s, lim_s, place_ref, *refs):
     n = len(segments)
     kv_refs = refs[:n]
-    o_ref, x_s, lim_s, o_s, q_s, m_s, acc_s, sa, sb = refs[n:]
+    o_ref, o_s, q_s, m_s, acc_s, sa, sb = refs[n:]
     z = info[0]
-    g = info[1]
-    length = info[2 + g]
-    cells = x_ref.shape[0] * x_ref.shape[1]
+    cells = x_s.shape[0]
     blocks, tok, _ = kv_refs[0].shape
     width = N_Z * tok
     cut = BATCH * STEPS
     rows = QH * cut
-    held, place_col = places_of_rows(z, g, length, cells, held_ref[0:1], held_ref[1:2])
-    index = lax.broadcasted_iota(jnp.int32, (cells, cells), 0).astype(jnp.float32)
-    pick = index == across(place_col)
-    x = x_ref[...].reshape(cells, FRESH_W)
-    x_s[...] = dot_nn(jnp.where(pick, 1.0, 0.0).astype(jnp.bfloat16), x).astype(jnp.bfloat16)
-    limits = jnp.sum(jnp.where(pick, across(held), 0.0), axis=1, keepdims=True)
-    lim_s[...] = jnp.broadcast_to(limits, (cells, 128))
     o_s[...] = jnp.zeros((cells, HEAD_W), jnp.bfloat16)
     places = lane_groups(key_slots(segments, z, N_Z, tok, 1).astype(jnp.float32))
 
@@ -274,14 +306,22 @@
         count = (most + width - 1) // width
         fill(sa, 0)
 
+        def two(j):
+            fill(sb, j + 1)
+            take(sa, j)
+            fill(sa, j + 2)
+            take(sb, j + 1)
+
         def body(i, carry):
-            fill(sb, 2 * i + 1)
-            take(sa, 2 * i)
-            fill(sa, 2 * i + 2)
-            take(sb, 2 * i + 1)
+            two(4 * i)
+            two(4 * i + 2)
             return carry
 
-        lax.fori_loop(0, count // 2, body, 0)
+        lax.fori_loop(0, count // 4, body, 0)
+
+        @pl.when(count % 4 >= 2)
+        def _():
+            two(count // 4 * 4)
 
         @pl.when(count % 2 == 1)
         def _():
@@ -292,20 +332,20 @@
             o_s[at, h * HD : (h + 1) * HD] = out[h * cut : (h + 1) * cut, :]
         return carry
 
-    owned = jnp.sum(jnp.where(held > 0.0, 1.0, 0.0)).astype(jnp.int32)
+    place = place_ref[:, 0:1]
+    owned = jnp.max(place_ref[...]).astype(jnp.int32) + 1
     lax.fori_loop(0, (owned + cut - 1) // cut, batch, 0)
-    index = lax.broadcasted_iota(jnp.int32, (cells, cells), 1).astype(jnp.float32)
-    put = (index == place_col) & (held > 0.0)
+    put = lax.broadcasted_iota(jnp.int32, (cells, cells), 1).astype(jnp.float32) == place
     out = dot_nn(jnp.where(put, 1.0, 0.0).astype(jnp.bfloat16), o_s[...]).astype(jnp.bfloat16)
     o_ref[...] = out.reshape(o_ref.shape)
 
 
-def verify(info, x, held, kvs, segments):
-    cells = x.shape[0] * x.shape[1]
+def verify(info, rows_in, shape, kvs, segments):
+    cells = rows_in[0].shape[0]
     rows = QH * BATCH * STEPS
     width = N_Z * kvs[0].shape[1]
-    operands = (x, held, *kvs)
-    out = jax.ShapeDtypeStruct((*x.shape[:2], HEAD_W), x.dtype)
+    operands = (*rows_in, *kvs)
+    out = jax.ShapeDtypeStruct((*shape[:2], HEAD_W), kvs[0].dtype)
     return pl.pallas_call(
         functools.partial(verify_kernel, tuple(segments)),
         out_shape=out,
@@ -315,8 +355,6 @@
             in_specs=[whole(a.shape) for a in operands],
             out_specs=whole(out.shape),
             scratch_shapes=[
-                pltpu.VMEM((cells, FRESH_W), jnp.bfloat16),
-                pltpu.VMEM((cells, 128), jnp.float32),
                 pltpu.VMEM((cells, HEAD_W), jnp.bfloat16),
                 pltpu.VMEM((rows, 2 * HD), jnp.bfloat16),
                 pltpu.VMEM((rows, 128), jnp.float32),
@@ -466,9 +504,10 @@
 
     info = jnp.concatenate([jnp.stack([z, g]), lengths]).astype(jnp.int32)
     held = jnp.stack([owner, cached])
+    rows_in = sort_rows(info, x, held)
     out = prefill(info, q, kvs, segments)
     out = exchange(out, XY)
-    decoded = verify(info, x, held, kvs, segments)
+    decoded = verify(info, rows_in, x.shape, kvs, segments)
     returned = exchange(decoded, GXY)
     return unpack_o(out), sum_rows(returned, rows, steps)
 

time: 117 us -> 114 us (0.974)
  the two profiles are of different devices: /device:TPU:2 before, /device:TPU:6 now
where the time goes in v4:
time: 114 us; the launch traced here: 112 us
  starting transfers between devices  51.9 us (46%)
  waiting for transfers between devices  36.5 us (32%)
  Pallas kernels  19.6 us (17%)
  local copies, waits for them, and re-layouts  3.59 us (3%)
    all_to_all x5, starting transfers between devices, exchange(): return lax.all_to_all(array, axes, 0, 0, tiled=True)  32.4 us
    all_to_all x5, waiting for transfers between devices, exchange(): return lax.all_to_all(array, axes, 0, 0, tiled=True)  23.7 us
    ppermute x8, starting transfers between devices, along(): return lax.ppermute(array, 'z', [(i, (i + shift) % zs) for i in range(zs)])  19.5 us
    ppermute x8, waiting for transfers between devices, along(): return lax.ppermute(array, 'z', [(i, (i + shift) % zs) for i in range(zs)])  12.8 us
    pallas_call x1, Pallas kernels, prefill(): pl.pallas_call(functools.partial(prefill_kernel, tuple(segments)), out_sh...  9.61 us
    unnamed x22, local copies, waits for them, and re-layouts  3.57 us
    pallas_call x1, Pallas kernels, verify(): pl.pallas_call(functools.partial(verify_kernel, tuple(segments)), out_sha...  3.4 us
  transfers between devices with their start and end apart: 13, of which 7 were waited for; matrix products, arithmetic and copies ran while one was open for 0% of the time, Pallas kernels for 15%

profile of v4, /device:TPU:6, one launch (start us, length us, event | category | flops | bytes accessed | tf_op | source)
XLA Modules:
  0.0 112.4 jit_solution(8844214961701647588)
XLA Ops:
  0.6 1.7 %pack_kv.1 = bf16[8,64,256]{2,1,0:T(8,128)(2,1)} custom-call(bf16[1,64,1024]{2,1,0:T(8,128)(2,1)} %k_ref.2, bf16[1,64,1024]{2,1,0:T(8,128)(2,1)} %v_ref.2), custom_call_target="tpu_custom_call" | custom-call | tf_op jit(solution)/shard_map/pack_kv/pallas_call | solution.py:382
  2.3 0.0 copy-start.1
  2.3 0.0 copy-start.2
  2.4 0.0 copy-start.3
  2.4 6.1 %all-to-all-start.1 = ((bf16[8,64,256]{2,1,0:T(8,128)(2,1)}), bf16[8,64,256]{2,1,0:T(8,128)(2,1)S(1)}, u32[]{:S(2)}, u32[]{:S(2)}) async-start(bf16[8,64,256]{2,1,0:T(8,128)(2,1)} %pack_kv.1), calls=%async_computation.1 | async-start | bytes 524288 | tf_op jit(solution)/shard_map/all_to_all | solution.py:489
  8.4 0.0 copy-done.1
  8.4 0.0 copy-done.2
  8.4 0.0 copy-done.3
  8.4 0.0 copy-start
  8.4 0.9 pack_rows.1
  9.3 4.9 %all-to-all-done.1.refs_0_ = bf16[8,64,256]{2,1,0:T(8,128)(2,1)S(1)} async-done(((bf16[8,64,256]{2,1,0:T(8,128)(2,1)}), bf16[8,64,256]{2,1,0:T(8,128)(2,1)S(1)}, u32[]{:S(2)}, u32[]{:S(2)}) %all-to-all-start.1) | async-done | bytes 262176 | tf_op jit(solution)/shard_map/all_to_all | solution.py:489
  14.2 5.9 %all-to-all-start.3 = ((bf16[32,8,1280]{2,1,0:T(8,128)(2,1)}), bf16[32,8,1280]{2,1,0:T(8,128)(2,1)S(1)}, u32[]{:S(2)}, u32[]{:S(2)}) async-start(bf16[32,8,1280]{2,1,0:T(8,128)(2,1)} %pack_rows.1), calls=%async_computation.3 | async-start | bytes 1310720 | tf_op jit(solution)/shard_map/all_to_all | solution.py:489
  20.1 5.9 %collective-permute-start.1 = (bf16[8,64,256]{2,1,0:T(8,128)(2,1)S(1)}, bf16[8,64,256]{2,1,0:T(8,128)(2,1)S(1)}, u32[]{:S(2)}, u32[]{:S(2)}) collective-permute-start(bf16[8,64,256]{2,1,0:T(8,128)(2,1)S(1)} %all-to-all-done.1.refs_0_), channel_id=1, source_target_pairs={{0,7},{1,0},{2,1},{3,2},{4,3},{5,4},{6,5},{7,6},{8,15},{9,8},{10,9... | collective-permute-start | bytes 786440 | tf_op jit(solution)/shard_map/ppermute | solution.py:486
  26.1 0.0 collective-permute-start
  26.1 0.0 copy-done
  26.1 1.0 pack_q.1
  27.1 4.3 %all-to-all-done.3.x_ref = bf16[32,8,1280]{2,1,0:T(8,128)(2,1)S(1)} async-done(((bf16[32,8,1280]{2,1,0:T(8,128)(2,1)}), bf16[32,8,1280]{2,1,0:T(8,128)(2,1)S(1)}, u32[]{:S(2)}, u32[]{:S(2)}) %all-to-all-start.3) | async-done | bytes 655392 | tf_op jit(solution)/shard_map/all_to_all | solution.py:489
  31.4 4.5 %all-to-all-start = ((bf16[8,64,1024]{2,1,0:T(8,128)(2,1)}), bf16[8,64,1024]{2,1,0:T(8,128)(2,1)S(1)}, u32[]{:S(2)}, u32[]{:S(2)}) async-start(bf16[8,64,1024]{2,1,0:T(8,128)(2,1)} %pack_q.1), calls=%async_computation | async-start | bytes 2097152 | tf_op jit(solution)/shard_map/all_to_all | solution.py:489
  35.9 0.0 collective-permute-done.1.refs_2_
  35.9 5.9 %collective-permute-start.3 = (bf16[8,64,256]{2,1,0:T(8,128)(2,1)S(1)}, bf16[8,64,256]{2,1,0:T(8,128)(2,1)S(1)}, u32[]{:S(2)}, u32[]{:S(2)}) collective-permute-start(bf16[8,64,256]{2,1,0:T(8,128)(2,1)S(1)} %collective-permute-done.1.refs_2_), channel_id=1, source_target_pairs={{0,7},{1,0},{2,1},{3,2},{4,3},{5,4},{6,5},{7,6},{8,15},{9,8},{10,9... | collective-permute-start | bytes 786440 | tf_op jit(solution)/shard_map/ppermute | solution.py:486
  41.7 0.0 collective-permute-done.refs_1_
  41.7 0.0 collective-permute-start.2
  41.7 4.8 %collective-permute-done.3.refs_4_ = bf16[8,64,256]{2,1,0:T(8,128)(2,1)S(1)} collective-permute-done((bf16[8,64,256]{2,1,0:T(8,128)(2,1)S(1)}, bf16[8,64,256]{2,1,0:T(8,128)(2,1)S(1)}, u32[]{:S(2)}, u32[]{:S(2)}) %collective-permute-start.3) | collective-permute-done | bytes 262176 | tf_op jit(solution)/shard_map/ppermute | solution.py:486
  46.5 3.7 %collective-permute-start.5 = (bf16[8,64,256]{2,1,0:T(8,128)(2,1)S(1)}, bf16[8,64,256]{2,1,0:T(8,128)(2,1)S(1)}, u32[]{:S(2)}, u32[]{:S(2)}) collective-permute-start(bf16[8,64,256]{2,1,0:T(8,128)(2,1)S(1)} %collective-permute-done.3.refs_4_), channel_id=1, source_target_pairs={{0,7},{1,0},{2,1},{3,2},{4,3},{5,4},{6,5},{7,6},{8,15},{9,8},{10,9... | collective-permute-start | bytes 786440 | tf_op jit(solution)/shard_map/ppermute | solution.py:486
  50.2 0.0 collective-permute-done.2.refs_3_
  50.2 0.0 collective-permute-start.4
  50.2 1.8 %collective-permute-start.7 = (bf16[8,32,256]{2,1,0:T(8,128)(2,1)S(1)}, bf16[8,32,256]{2,1,0:T(8,128)(2,1)S(1)}, u32[]{:S(2)}, u32[]{:S(2)}) collective-permute-start(bf16[8,32,256]{2,1,0:T(8,128)(2,1)S(1)} %slice.9), channel_id=1, source_target_pairs={{0,5},{1,6},{2,7},{3,0},{4,1},{5,2},{6,3},{7,4},{8,13},{9,14},{10,... | collective-permute-start | bytes 393224 | tf_op jit(solution)/shard_map/ppermute | solution.py:486
  52.0 2.2 %collective-permute-start.6 = (bf16[8,32,256]{2,1,0:T(8,128)(2,1)S(1)}, bf16[8,32,256]{2,1,0:T(8,128)(2,1)S(1)}, u32[]{:S(2)}, u32[]{:S(2)}) collective-permute-start(bf16[8,32,256]{2,1,0:T(8,128)(2,1)S(1)} %slice.8), channel_id=1, source_target_pairs={{0,3},{1,4},{2,5},{3,6},{4,7},{5,0},{6,1},{7,2},{8,11},{9,12},{10,... | collective-permute-start | bytes 393224 | tf_op jit(solution)/shard_map/ppermute | solution.py:486
  54.2 0.0 copy-start.10
  54.2 0.7 copy-done.10
  54.9 0.0 copy-start.9
  54.9 0.1 pad_add_fusion.1.info
  55.0 0.0 copy-start.8
  55.0 0.6 copy-done.9
  55.6 0.1 copy-done.8
  55.7 1.2 %sort_rows.1 = (bf16[256,1280]{1,0:T(8,128)(2,1)S(1)}, f32[256,128]{1,0:T(8,128)S(1)}, f32[256,128]{1,0:T(8,128)S(1)}) custom-call(s32[6]{0:T(128)S(1)} %pad_add_fusion.1.info, bf16[32,8,1280]{2,1,0:T(8,128)(2,1)S(1)} %all-to-all-done.3.x_ref, s32[2,512]{1,0:T(2,128)S(1)} %pad_add_fusion.held_ref), custom_call_target="tpu_custom_call" | custom-call | tf_op jit(solution)/shard_map/sort_rows/pallas_call | solution.py:252
  56.9 5.8 %collective-permute-done.7.refs_8_ = bf16[8,32,256]{2,1,0:T(8,128)(2,1)S(1)} collective-permute-done((bf16[8,32,256]{2,1,0:T(8,128)(2,1)S(1)}, bf16[8,32,256]{2,1,0:T(8,128)(2,1)S(1)}, u32[]{:S(2)}, u32[]{:S(2)}) %collective-permute-start.7) | collective-permute-done | bytes 131104 | tf_op jit(solution)/shard_map/ppermute | solution.py:486
  62.6 0.5 collective-permute-done.6.refs_7_
  63.1 0.0 collective-permute-done.5.refs_6_
  63.1 1.8 %collective-permute-done.4.refs_5_ = bf16[8,64,256]{2,1,0:T(8,128)(2,1)S(1)} collective-permute-done((bf16[8,64,256]{2,1,0:T(8,128)(2,1)S(1)}, bf16[8,64,256]{2,1,0:T(8,128)(2,1)S(1)}, u32[]{:S(2)}, u32[]{:S(2)}) %collective-permute-start.4) | collective-permute-done | bytes 262176 | tf_op jit(solution)/shard_map/ppermute | solution.py:486
  64.8 3.4 %verify.1 = bf16[32,8,1024]{2,1,0:T(8,128)(2,1)} custom-call(s32[6]{0:T(128)S(1)} %pad_add_fusion.1.info, bf16[256,1280]{1,0:T(8,128)(2,1)S(1)} %get-tuple-element.5.x_s, f32[256,128]{1,0:T(8,128)S(1)} %get-tuple-element.6.lim_s, f32[256,128]{1,0:T(8,128)S(1)} %get-tuple-element.7.place_ref, bf16[8,64,256]{2,1,0:T(8,128)(2,1)S(1)} %all-to-all-done.1.refs_0_, ...), custom_call_target="tpu_custom_call" | custom-call | flops 4000000000 | bytes 4194304 | tf_op jit(solution)/shard_map/verify/pallas_call | solution.py:349
  68.2 0.0 copy-start.4
  68.2 0.7 copy-done.4
  68.9 0.0 copy-start.6
  68.9 0.7 copy-done.6
  69.5 0.0 all-to-all-done.q_ref
  69.6 0.0 copy-start.5
  69.6 10.3 %all-to-all-start.4 = ((bf16[32,8,1024]{2,1,0:T(8,128)(2,1)}), bf16[32,8,1024]{2,1,0:T(8,128)(2,1)S(1)}, u32[]{:S(2)}, u32[]{:S(2)}) async-start(bf16[32,8,1024]{2,1,0:T(8,128)(2,1)} %verify.1), calls=%async_computation.4 | async-start | bytes 1048576 | tf_op jit(solution)/shard_map/all_to_all | solution.py:489
  79.8 0.0 copy-done.5
  79.9 0.0 copy-start.7
  79.9 0.9 copy-done.7
  80.8 9.6 %prefill.1 = bf16[8,64,1024]{2,1,0:T(8,128)(2,1)} custom-call(s32[6]{0:T(128)S(1)} %pad_add_fusion.1.info, bf16[8,64,1024]{2,1,0:T(8,128)(2,1)S(1)} %all-to-all-done.q_ref, bf16[8,64,256]{2,1,0:T(8,128)(2,1)S(1)} %all-to-all-done.1.refs_0_, bf16[8,64,256]{2,1,0:T(8,128)(2,1)S(1)} %collective-permute-done.refs_1_, ...), custom_call_target="tpu_custom_call" | custom-call | flops 20000000000 | bytes 4194304 | tf_op jit(solution)/shard_map/prefill/pallas_call | solution.py:184
  90.4 0.0 all-to-all-done.4.x_ref
  90.4 5.7 %all-to-all-start.2 = ((bf16[8,64,1024]{2,1,0:T(8,128)(2,1)}), bf16[8,64,1024]{2,1,0:T(8,128)(2,1)S(1)}, u32[]{:S(2)}, u32[]{:S(2)}) async-start(bf16[8,64,1024]{2,1,0:T(8,128)(2,1)} %prefill.1), calls=%async_computation.2 | async-start | bytes 2097152 | tf_op jit(solution)/shard_map/all_to_all | solution.py:489
  96.1 0.7 sum_rows.1
  96.8 14.5 %all-to-all-done.2.x_ref = bf16[8,64,1024]{2,1,0:T(8,128)(2,1)S(1)} async-done(((bf16[8,64,1024]{2,1,0:T(8,128)(2,1)}), bf16[8,64,1024]{2,1,0:T(8,128)(2,1)S(1)}, u32[]{:S(2)}, u32[]{:S(2)}) %all-to-all-start.2) | async-done | bytes 1048608 | tf_op jit(solution)/shard_map/all_to_all | solution.py:489
  111.4 1.0 unpack_o.1
  (3 shorter events, 0.0 us)
Async XLA Ops:
  2.3 6.1 %copy-start.1 = (bf16[2,4,8192]{2,1,0:T(4,128)(2,1)S(1)}, bf16[2,4,8192]{2,1,0:T(4,128)(2,1)}, u32[]{:S(2)}) copy-start(bf16[2,4,8192]{2,1,0:T(4,128)(2,1)} %q_ref.1) | copy-start | bytes 393220
  2.3 6.1 %copy-start.2 = (bf16[2,4,1024]{2,1,0:T(4,128)(2,1)S(1)}, bf16[2,4,1024]{2,1,0:T(4,128)(2,1)}, u32[]{:S(2)}) copy-start(bf16[2,4,1024]{2,1,0:T(4,128)(2,1)} %k_ref.3) | copy-start | bytes 49156
  2.4 6.1 %copy-start.3 = (bf16[2,4,1024]{2,1,0:T(4,128)(2,1)S(1)}, bf16[2,4,1024]{2,1,0:T(4,128)(2,1)}, u32[]{:S(2)}) copy-start(bf16[2,4,1024]{2,1,0:T(4,128)(2,1)} %v_ref.3) | copy-start | bytes 49156
  2.4 11.9 %all-to-all-start.1 = ((bf16[8,64,256]{2,1,0:T(8,128)(2,1)}), bf16[8,64,256]{2,1,0:T(8,128)(2,1)S(1)}, u32[]{:S(2)}, u32[]{:S(2)}) async-start(bf16[8,64,256]{2,1,0:T(8,128)(2,1)} %pack_kv.1), calls=%async_computation.1 | async-start | bytes 524288 | tf_op jit(solution)/shard_map/all_to_all | solution.py:489
  8.4 17.6 %copy-start = (bf16[1,64,8192]{2,1,0:T(8,128)(2,1)S(1)}, bf16[1,64,8192]{2,1,0:T(8,128)(2,1)}, u32[]{:S(2)}) copy-start(bf16[1,64,8192]{2,1,0:T(8,128)(2,1)} %x_ref.1) | copy-start | bytes 3145732
  14.2 17.2 %all-to-all-start.3 = ((bf16[32,8,1280]{2,1,0:T(8,128)(2,1)}), bf16[32,8,1280]{2,1,0:T(8,128)(2,1)S(1)}, u32[]{:S(2)}, u32[]{:S(2)}) async-start(bf16[32,8,1280]{2,1,0:T(8,128)(2,1)} %pack_rows.1), calls=%async_computation.3 | async-start | bytes 1310720 | tf_op jit(solution)/shard_map/all_to_all | solution.py:489
  20.1 15.7 %collective-permute-start.1 = (bf16[8,64,256]{2,1,0:T(8,128)(2,1)S(1)}, bf16[8,64,256]{2,1,0:T(8,128)(2,1)S(1)}, u32[]{:S(2)}, u32[]{:S(2)}) collective-permute-start(bf16[8,64,256]{2,1,0:T(8,128)(2,1)S(1)} %all-to-all-done.1.refs_0_), channel_id=1, source_target_pairs={{0,7},{1,0},{2,1},{3,2},{4,3},{5,4},{6,5},{7,6},{8,15},{9,8},{10,9... | collective-permute-start | bytes 786440 | tf_op jit(solution)/shard_map/ppermute | solution.py:486
  26.1 15.7 %collective-permute-start = (bf16[8,64,256]{2,1,0:T(8,128)(2,1)S(1)}, bf16[8,64,256]{2,1,0:T(8,128)(2,1)S(1)}, u32[]{:S(2)}, u32[]{:S(2)}) collective-permute-start(bf16[8,64,256]{2,1,0:T(8,128)(2,1)S(1)} %all-to-all-done.1.refs_0_), channel_id=1, source_target_pairs={{0,1},{1,2},{2,3},{3,4},{4,5},{5,6},{6,7},{7,0},{8,9},{9,10},{10,1... | collective-permute-start | bytes 786440 | tf_op jit(solution)/shard_map/ppermute | solution.py:486
  31.4 38.2 %all-to-all-start = ((bf16[8,64,1024]{2,1,0:T(8,128)(2,1)}), bf16[8,64,1024]{2,1,0:T(8,128)(2,1)S(1)}, u32[]{:S(2)}, u32[]{:S(2)}) async-start(bf16[8,64,1024]{2,1,0:T(8,128)(2,1)} %pack_q.1), calls=%async_computation | async-start | bytes 2097152 | tf_op jit(solution)/shard_map/all_to_all | solution.py:489
  35.9 10.7 %collective-permute-start.3 = (bf16[8,64,256]{2,1,0:T(8,128)(2,1)S(1)}, bf16[8,64,256]{2,1,0:T(8,128)(2,1)S(1)}, u32[]{:S(2)}, u32[]{:S(2)}) collective-permute-start(bf16[8,64,256]{2,1,0:T(8,128)(2,1)S(1)} %collective-permute-done.1.refs_2_), channel_id=1, source_target_pairs={{0,7},{1,0},{2,1},{3,2},{4,3},{5,4},{6,5},{7,6},{8,15},{9,8},{10,9... | collective-permute-start | bytes 786440 | tf_op jit(solution)/shard_map/ppermute | solution.py:486
  41.7 8.5 %collective-permute-start.2 = (bf16[8,64,256]{2,1,0:T(8,128)(2,1)S(1)}, bf16[8,64,256]{2,1,0:T(8,128)(2,1)S(1)}, u32[]{:S(2)}, u32[]{:S(2)}) collective-permute-start(bf16[8,64,256]{2,1,0:T(8,128)(2,1)S(1)} %collective-permute-done.refs_1_), channel_id=1, source_target_pairs={{0,1},{1,2},{2,3},{3,4},{4,5},{5,6},{6,7},{7,0},{8,9},{9,10},{10,1... | collective-permute-start | bytes 786440 | tf_op jit(solution)/shard_map/ppermute | solution.py:486
  46.5 16.5 %collective-permute-start.5 = (bf16[8,64,256]{2,1,0:T(8,128)(2,1)S(1)}, bf16[8,64,256]{2,1,0:T(8,128)(2,1)S(1)}, u32[]{:S(2)}, u32[]{:S(2)}) collective-permute-start(bf16[8,64,256]{2,1,0:T(8,128)(2,1)S(1)} %collective-permute-done.3.refs_4_), channel_id=1, source_target_pairs={{0,7},{1,0},{2,1},{3,2},{4,3},{5,4},{6,5},{7,6},{8,15},{9,8},{10,9... | collective-permute-start | bytes 786440 | tf_op jit(solution)/shard_map/ppermute | solution.py:486
  50.2 14.6 %collective-permute-start.4 = (bf16[8,64,256]{2,1,0:T(8,128)(2,1)S(1)}, bf16[8,64,256]{2,1,0:T(8,128)(2,1)S(1)}, u32[]{:S(2)}, u32[]{:S(2)}) collective-permute-start(bf16[8,64,256]{2,1,0:T(8,128)(2,1)S(1)} %collective-permute-done.2.refs_3_), channel_id=1, source_target_pairs={{0,1},{1,2},{2,3},{3,4},{4,5},{5,6},{6,7},{7,0},{8,9},{9,10},{10,1... | collective-permute-start | bytes 786440 | tf_op jit(solution)/shard_map/ppermute | solution.py:486
  50.2 12.4 %collective-permute-start.7 = (bf16[8,32,256]{2,1,0:T(8,128)(2,1)S(1)}, bf16[8,32,256]{2,1,0:T(8,128)(2,1)S(1)}, u32[]{:S(2)}, u32[]{:S(2)}) collective-permute-start(bf16[8,32,256]{2,1,0:T(8,128)(2,1)S(1)} %slice.9), channel_id=1, source_target_pairs={{0,5},{1,6},{2,7},{3,0},{4,1},{5,2},{6,3},{7,4},{8,13},{9,14},{10,... | collective-permute-start | bytes 393224 | tf_op jit(solution)/shard_map/ppermute | solution.py:486
  52.0 11.0 %collective-permute-start.6 = (bf16[8,32,256]{2,1,0:T(8,128)(2,1)S(1)}, bf16[8,32,256]{2,1,0:T(8,128)(2,1)S(1)}, u32[]{:S(2)}, u32[]{:S(2)}) collective-permute-start(bf16[8,32,256]{2,1,0:T(8,128)(2,1)S(1)} %slice.8), channel_id=1, source_target_pairs={{0,3},{1,4},{2,5},{3,6},{4,7},{5,0},{6,1},{7,2},{8,11},{9,12},{10,... | collective-permute-start | bytes 393224 | tf_op jit(solution)/shard_map/ppermute | solution.py:486
  54.2 0.7 copy-start.10
  54.9 0.7 copy-start.9
  55.0 0.7 copy-start.8
  68.2 0.7 copy-start.4
  68.9 0.7 copy-start.6
  69.6 10.3 %copy-start.5 = (bf16[8,32,256]{2,1,0:T(8,128)(2,1)S(1)}, bf16[8,32,256]{2,1,0:T(8,128)(2,1)}, u32[]{:S(2)}) copy-start(bf16[8,32,256]{2,1,0:T(8,128)(2,1)} %copy-done.4) | copy-start | bytes 393220
  69.6 20.8 %all-to-all-start.4 = ((bf16[32,8,1024]{2,1,0:T(8,128)(2,1)}), bf16[32,8,1024]{2,1,0:T(8,128)(2,1)S(1)}, u32[]{:S(2)}, u32[]{:S(2)}) async-start(bf16[32,8,1024]{2,1,0:T(8,128)(2,1)} %verify.1), calls=%async_computation.4 | async-start | bytes 1048576 | tf_op jit(solution)/shard_map/all_to_all | solution.py:489
  79.9 0.9 copy-start.7
  90.4 21.0 %all-to-all-start.2 = ((bf16[8,64,1024]{2,1,0:T(8,128)(2,1)}), bf16[8,64,1024]{2,1,0:T(8,128)(2,1)S(1)}, u32[]{:S(2)}, u32[]{:S(2)}) async-start(bf16[8,64,1024]{2,1,0:T(8,128)(2,1)} %prefill.1), calls=%async_computation.2 | async-start | bytes 2097152 | tf_op jit(solution)/shard_map/all_to_all | solution.py:489
